TPU v7x, 128 devices: a whole 4x4x4 slice. The times are simulated.
128 devices in a mesh: dp: 16 (over x_lo, y, core), mp: 8 (over x_hi, z).
Axes of the slice: x: 4 (x_hi: 2, x_lo: 2; x = x_hi * 2 + x_lo), y: 4, z: 4, core: 2. Of those that a mesh axis runs over, the one named last changes fastest.
Arguments:
- tokens: bfloat16 [4096, 6144], P('dp', 'mp'), may hold values from -40 to 40
- norm_gain: float32 [6144], P('mp'), may hold values from 0.1 to 1.9
- w_qkv: bfloat16 [6144, 3, 4096], P('mp', None, 'dp'), may hold values from -0.078125 to 0.078125
- w_up: bfloat16 [6144, 12288], P('mp', 'dp'), may hold values from -0.078125 to 0.078125
- w_attn_out: bfloat16 [4096, 6144], P('dp', 'mp'), may hold values from -0.09375 to 0.09375
- w_down: bfloat16 [12288, 6144], P('dp', 'mp'), may hold values from -0.0546875 to 0.0546875
Outputs:
- layer_out: bfloat16 [4096, 6144], P('dp', 'mp')
All inputs are finite; a program needn't handle non-finite values.
Results may differ from a plain program's by a relative error of at most 0.015.
Values may be sent and summed in bfloat16 or wider, within the bound.
A program may use at most 128 MiB of HBM per device.

v0:
```python
import jax
import jax.numpy as jnp
from jax import lax
from jax.sharding import Mesh
from jax.sharding import PartitionSpec as P

HEAD_DIM = 128
PATCHES = 256
DP = ("dp_0", "dp_1", "dp_2")


EPS = 1e-06


def sent_to_all(array, axis):
    length = lax.axis_size(axis)
    return lax.all_to_all(
        jnp.broadcast_to(array[None], (length, *array.shape)), axis, 0, 0, tiled=True
    )


def over_copies(array, axis):
    return sent_to_all(array, axis).sum(axis=0)


def in_one(arrays, axis):
    vector, at, finished = (jnp.concatenate([a.reshape(-1) for a in arrays]), 0, [])
    running = over_copies(vector, axis)
    for a in arrays:
        finished.append(running[at : at + a.size].reshape(a.shape))
        at += a.size
    return tuple(finished)


def split_up(array, dim, length):
    lengths = array.shape
    parts = array.reshape(*lengths[:dim], length, lengths[dim] // length, *lengths[dim + 1 :])
    return jnp.moveaxis(parts, dim, 0)


def sum_by_chip(array, chips, core, dim):
    sizes = (lax.axis_size(chips), lax.axis_size(core))
    parts = split_up(array, dim, sizes[0] * sizes[1])
    inside = parts.shape[1:]
    parts = parts.reshape(*sizes, *inside).swapaxes(0, 1).reshape(-1, *inside)
    parts = lax.psum_scatter(parts, core, scatter_dimension=0, tiled=True)
    return lax.psum_scatter(parts, chips, scatter_dimension=0, tiled=True)[0]


def normalize_rows(values, total, squares, gain, width):
    mean = total / width
    spread = squares / width - mean * mean
    scaled = (values - mean[:, None]) * lax.rsqrt(spread + EPS)[:, None]
    return (scaled * gain[None, :]).astype(jnp.bfloat16)


def head_norm(values):
    mean = jnp.mean(values, axis=-1, keepdims=True)
    centered = values - mean
    spread = jnp.mean(centered * centered, axis=-1, keepdims=True)
    return centered * lax.rsqrt(spread + EPS)


def attend(qkv, heads_here):
    rows = qkv.shape[0]
    images = rows // PATCHES
    parts = qkv.reshape(images, PATCHES, 3, heads_here, HEAD_DIM)
    query = (head_norm(parts[:, :, 0].astype(jnp.float32)) * (1.0 / HEAD_DIM) ** 0.5).astype(
        jnp.bfloat16
    )
    keys = head_norm(parts[:, :, 1].astype(jnp.float32)).astype(jnp.bfloat16)
    values = parts[:, :, 2]
    scores = jnp.einsum("iqhd,ikhd->ihqk", query, keys, preferred_element_type=jnp.float32)
    weights = jnp.exp(scores)
    probs = (weights / jnp.sum(weights, axis=-1, keepdims=True)).astype(jnp.bfloat16)
    mixed = jnp.einsum("ihqk,ikhd->iqhd", probs, values, preferred_element_type=jnp.float32)
    return mixed.astype(jnp.bfloat16).reshape(rows, heads_here * HEAD_DIM)


def local(tokens, norm_gain, w_qkv, w_up, w_attn_out, w_down):
    n_mp = lax.axis_size("mp")
    feat_here = tokens.shape[1]
    head_cols = w_qkv.shape[2]
    heads_here = head_cols // HEAD_DIM
    width = feat_here * n_mp
    tokens_f = tokens.astype(jnp.float32)
    total, squares = in_one((jnp.sum(tokens_f, axis=1), jnp.sum(tokens_f * tokens_f, axis=1)), "mp")
    normed = normalize_rows(tokens_f, total, squares, norm_gain, width)
    normed_all = lax.all_gather(normed, DP, axis=0, tiled=True)
    w_heads = w_qkv.reshape(feat_here, 3 * head_cols)
    projected = lax.psum_scatter(
        jnp.concatenate(
            [
                jnp.dot(normed_all, w_heads, preferred_element_type=jnp.float32),
                jnp.dot(normed_all, w_up, preferred_element_type=jnp.float32),
            ],
            axis=1,
        ).astype(jnp.bfloat16),
        "mp",
        scatter_dimension=0,
        tiled=True,
    )
    qkv = projected[:, : 3 * head_cols].reshape(projected.shape[0], 3, head_cols)
    attended = attend(qkv, heads_here)
    activated = jax.nn.gelu(projected[:, 3 * head_cols :].astype(jnp.float32)).astype(jnp.bfloat16)
    hidden = jnp.concatenate([attended, activated], axis=1)
    piece = lax.all_gather(hidden, "mp", axis=0, tiled=True)
    result = jnp.dot(piece[:, :head_cols], w_attn_out, preferred_element_type=jnp.float32)
    partial_out = result + jnp.dot(piece[:, head_cols:], w_down, preferred_element_type=jnp.float32)
    summed = sum_by_chip(partial_out.astype(jnp.bfloat16), ("dp_0", "dp_1"), "dp_2", 0).astype(
        jnp.float32
    )
    return (tokens_f + summed).astype(jnp.bfloat16)


def solution(mesh):
    torus = Mesh(mesh.devices.reshape(2, 4, 2, mesh.shape["mp"]), ("dp_0", "dp_1", "dp_2", "mp"))
    in_specs = (P(DP, "mp"), P("mp"), P("mp", None, DP), P("mp", DP), P(DP, "mp"), P(DP, "mp"))
    out_specs = P(DP, "mp")
    return jax.shard_map(local, mesh=torus, in_specs=in_specs, out_specs=out_specs, check_vma=False)
```

profile of v0, /device:TPU:1, one launch (start us, length us, event | category | flops | bytes accessed | tf_op | source)
XLA Modules:
  0.0 445.0 jit_solution(9964850077042183659)
XLA Ops:
  6.5 1.3 convert_reduce_fusion
  7.9 14.7 %all_to_all.6 = f32[8,1,512]{2,1,0:T(1,128)S(1)} all-to-all(f32[8,1,512]{2,1,0:T(1,128)S(1)} %broadcast_in_dim.2), channel_id=1, replica_groups=mesh['dp_0'=2,'dp_1'=4,'dp_2'=2,'mp'=8] {'mp'}, dimensions={0} | all-to-all | bytes 32768 | tf_op jit(solution)/shard_map/all_to_all | solution.py:17
  22.6 2.0 fusion.13
  24.7 1.6 copy.28
  26.2 39.7 %all-gather.3.cloned.1.call-done = bf16[4096,768]{1,0:T(8,128)(2,1)} async-done(((bf16[256,768]{1,0:T(8,128)(2,1)}), bf16[4096,768]{1,0:T(8,128)(2,1)}) %all-gather.3.cloned.1.call-update) | async-done | bytes 6291472 | tf_op jit(solution)/shard_map/all_gather | solution.py:89
  66.0 8.2 %convolution_convert_fusion.1 = bf16[4096,768]{0,1:T(8,128)(2,1)S(1)} fusion(bf16[4096,768]{1,0:T(8,128)(2,1)} %all-gather.3.cloned.1.call-done, bf16[768,768]{0,1:T(8,128)(2,1)S(1)} %bitcast.57), kind=kOutput, calls=%fused_computation.3 | convolution fusion | flops 4834983936 | bytes 13762560 | tf_op jit(solution)/shard_map/dot_general | solution.py:94
  74.2 5.3 %convolution_convert_fusion = bf16[4096,768]{0,1:T(8,128)(2,1)S(1)} fusion(bf16[4096,768]{1,0:T(8,128)(2,1)S(1)} %copy-done.5, bf16[768,768]{1,0:T(8,128)(2,1)S(1)} %copy-done), kind=kOutput, calls=%fused_computation.2 | convolution fusion | flops 4834983936 | bytes 13762560 | tf_op jit(solution)/shard_map/dot_general | solution.py:95
  79.6 11.1 %pad_maximum_fusion = bf16[4096,1536]{0,1:T(8,128)(2,1)} fusion(bf16[4096,768]{0,1:T(8,128)(2,1)S(1)} %convolution_convert_fusion, bf16[4096,768]{0,1:T(8,128)(2,1)S(1)} %convolution_convert_fusion.1), kind=kLoop, calls=%fused_computation | loop fusion | flops 25165824 | bytes 25165824 | tf_op jit(solution)/shard_map/concatenate | solution.py:92
  90.7 0.0 all-gather.5.cloned.1.call-start
  90.7 150.8 %reduce-scatter.4.cloned.1.call-done = bf16[512,1536]{0,1:T(8,128)(2,1)} async-done(((bf16[4096,1536]{0,1:T(8,128)(2,1)}), bf16[512,1536]{0,1:T(8,128)(2,1)}) %reduce-scatter.4.cloned.1.call-update) | async-done | bytes 1572880 | tf_op jit(solution)/shard_map/reduce_scatter | solution.py:91
  241.5 1.2 slice.36
  242.7 0.2 reshape_reshape.6
  242.9 0.5 fusion.36
  243.4 0.2 copy.41
  243.7 0.2 convert_reduce_fusion.1
  243.8 0.4 fusion.24
  244.2 0.2 copy.40
  244.4 0.2 convert_reduce_fusion.2
  244.6 0.4 fusion.18
  245.0 1.4 convolution_exponential_fusion
  246.4 0.3 fusion.9
  246.7 0.3 copy.33
  247.1 0.5 fusion.8
  247.6 1.1 pad_maximum_fusion.1
  248.8 0.2 reduce-scatter.6.cloned.1.call-start
  249.0 110.3 %all-gather.5.cloned.1.call-done = bf16[4096,1024]{0,1:T(8,128)(2,1)} async-done(((bf16[512,1024]{0,1:T(8,128)(2,1)}), bf16[4096,1024]{0,1:T(8,128)(2,1)}) %all-gather.5.cloned.1.call-update) | async-done | bytes 8388624 | tf_op jit(solution)/shard_map/all_gather | solution.py:107
  359.3 7.8 %fusion = f32[4096,768]{1,0:T(8,128)S(1)} fusion(bf16[768,768]{1,0:T(8,128)(2,1)} %param.11, bf16[4096,1024]{0,1:T(8,128)(2,1)} %all-gather.5.cloned.1.call-done), kind=kOutput, calls=%fused_computation.4 | convolution fusion | flops 4831838208 | bytes 20054016 | tf_op jit(solution)/shard_map/dot_general | solution.py:109
  367.1 3.7 add_convert_fusion
  370.8 3.1 copy.34
  374.0 15.6 %reduce-scatter.6.cloned.1.call-done = bf16[8,256,768]{2,1,0:T(8,128)(2,1)} async-done(((bf16[16,256,768]{2,1,0:T(8,128)(2,1)}), bf16[8,256,768]{2,1,0:T(8,128)(2,1)}) %reduce-scatter.6.cloned.1.call-update) | async-done | bytes 3145744 | tf_op jit(solution)/shard_map/reduce_scatter | solution.py:46
  389.7 47.0 %reduce-scatter.8.cloned.1.call-done = bf16[1,256,768]{2,1,0:T(8,128)(2,1)} async-done(((bf16[8,256,768]{2,1,0:T(8,128)(2,1)}), bf16[1,256,768]{2,1,0:T(8,128)(2,1)}) %reduce-scatter.8.cloned.1.call-update) | async-done | bytes 393232 | tf_op jit(solution)/shard_map/reduce_scatter | solution.py:47
  436.6 1.8 fusion.14
  (28 shorter events, 0.3 us)
Async XLA Ops:
  6.5 67.7 %copy-start = (bf16[768,768]{1,0:T(8,128)(2,1)S(1)}, bf16[768,768]{1,0:T(8,128)(2,1)}, u32[]{:S(2)}) copy-start(bf16[768,768]{1,0:T(8,128)(2,1)} %param.9) | copy-start | bytes 3538948
  6.5 59.4 %all-gather.3.cloned.1.call-start = ((), (), s32[]{:S(2)}) async-start(), calls=%async_computation.4 | async-start | bytes 6684672 | tf_op jit(solution)/shard_map/all_gather | solution.py:89
  24.6 216.9 %reduce-scatter.4.cloned.1.call-start = ((), (), s32[]{:S(2)}) async-start(), calls=%async_computation.5 | async-start | bytes 14155776 | tf_op jit(solution)/shard_map/reduce_scatter | solution.py:91
  66.0 8.2 %copy-start.5 = (bf16[4096,768]{1,0:T(8,128)(2,1)S(1)}, bf16[4096,768]{1,0:T(8,128)(2,1)}, u32[]{:S(2)}) copy-start(bf16[4096,768]{1,0:T(8,128)(2,1)} %all-gather.3.cloned.1.call-done) | copy-start | bytes 18874372
  90.7 268.6 %all-gather.5.cloned.1.call-start = ((), (), s32[]{:S(2)}) async-start(), calls=%async_computation.6 | async-start | bytes 9437184 | tf_op jit(solution)/shard_map/all_gather | solution.py:107
  242.7 4.4 copy-start.3
  248.8 118.3 %copy-start.4 = (bf16[256,768]{1,0:T(8,128)(2,1)S(1)}, bf16[256,768]{1,0:T(8,128)(2,1)}, u32[]{:S(2)}) copy-start(bf16[256,768]{1,0:T(8,128)(2,1)} %param.10) | copy-start | bytes 1179652
  248.8 140.8 %reduce-scatter.6.cloned.1.call-start = ((), (), s32[]{:S(2)}) async-start(), calls=%async_computation.7 | async-start | bytes 9437184 | tf_op jit(solution)/shard_map/reduce_scatter | solution.py:46
  370.8 67.7 %copy-start.1 = (bf16[768,768]{1,0:T(8,128)(2,1)S(1)}, bf16[768,768]{1,0:T(8,128)(2,1)}, u32[]{:S(2)}) copy-start(bf16[768,768]{1,0:T(8,128)(2,1)} %param.9) | copy-start | bytes 3538948
  373.9 62.7 %copy-start.2 = (bf16[256,768]{1,0:T(8,128)(2,1)S(1)}, bf16[256,768]{1,0:T(8,128)(2,1)}, u32[]{:S(2)}) copy-start(bf16[256,768]{1,0:T(8,128)(2,1)} %param.6) | copy-start | bytes 1179652
  373.9 62.7 %reduce-scatter.8.cloned.1.call-start = ((), (), s32[]{:S(2)}) async-start(), calls=%async_computation.8 | async-start | bytes 3538944 | tf_op jit(solution)/shard_map/reduce_scatter | solution.py:47
Sparse Core Ops, SparseCore 0:
  24.7 41.1 all-gather.2
  90.8 150.6 reduce-scatter.3
  248.9 110.4 all-gather.4
  374.1 15.5 reduce-scatter.5
  391.9 44.6 reduce-scatter.7
where the time goes:
time: 448 us; the launch traced here: 445 us
  waiting for transfers between devices  363 us (81%)
  matrix products  26.7 us (6%)
  other arithmetic  19.1 us (4%)
  blocking collectives  14.7 us (3%)
  between operations  13.3 us (3%)
  local copies, waits for them, and re-layouts  7.36 us (2%)
    reduce_scatter x1, waiting for transfers between devices, local(): lax.psum_scatter(jnp.concatenate([jnp.dot(normed_all, w_heads, preferred_...  151 us
    all_gather x1, waiting for transfers between devices, local(): piece = lax.all_gather(hidden, 'mp', axis=0, tiled=True)  110 us
    reduce_scatter x1, waiting for transfers between devices, sum_by_chip(): return lax.psum_scatter(parts, chips, scatter_dimension=0, tiled=True)[0]  47 us
    all_gather x1, waiting for transfers between devices, local(): normed_all = lax.all_gather(normed, DP, axis=0, tiled=True)  39.7 us
    reduce_scatter x1, waiting for transfers between devices, sum_by_chip(): parts = lax.psum_scatter(parts, core, scatter_dimension=0, tiled=True)  15.6 us
    all_to_all x1, blocking collectives, sent_to_all(): lax.all_to_all(jnp.broadcast_to(array[None], (length, *array.shape)), axi...  14.7 us
    concatenate x1, other arithmetic, local(): jnp.concatenate([jnp.dot(normed_all, w_heads, preferred_element_type=jnp....  11.1 us
  transfers between devices with their start and end apart: 5, of which 5 were waited for; matrix products, arithmetic and copies ran while one was open for 0% of the time, Pallas kernels for 0%

commit v1 on v0

v1 whole, which is shorter than its diff:
```python
import functools

import jax
import jax.numpy as jnp
from jax import lax
from jax.experimental import pallas as pl
from jax.experimental.pallas import tpu as pltpu
from jax.sharding import Mesh
from jax.sharding import PartitionSpec as P

HEAD_DIM = 128
PATCHES = 256
EPS = 1e-06
MESH = pl.DeviceIdType.MESH
F32 = jnp.float32
BF16 = jnp.bfloat16
DP = ("L", "Y", "C")
MP = ("H", "Z")

CHUNKS = 3
RELS = (2, 1, 3, 0)
N_SEND = 160
N_RECV = 160


def gelu(u):
    return 0.5 * u * (1.0 + jnp.tanh(0.7978845608028654 * (u + 0.044715 * (u * u * u))))


def head_norm(values):
    mean = jnp.mean(values, axis=-1, keepdims=True)
    centered = values - mean
    spread = jnp.mean(centered * centered, axis=-1, keepdims=True)
    return centered * lax.rsqrt(spread + EPS)


def kernel(
    width,
    tok, stats, gain, w1, w_attn, w_down,
    out,
    statbuf, normed, xbuf, w1buf, w2buf, pbuf, r1, r2, qkv, hbuf, obuf, osend, osib, ry1, ry2, xsend, xrecv,
    send_sem, recv_sem,
):
    L, Y, C, H, Z = (lax.axis_index(a) for a in ("L", "Y", "C", "H", "Z"))
    rows, feat = tok.shape
    half = rows // 2
    wide = pbuf.shape[-1]
    lo = {"L": 1 - L}
    cross = {"L": 1 - L, "H": 1 - H}
    up, down = {"Y": lax.rem(Y + 1, 4)}, {"Y": lax.rem(Y + 3, 4)}
    fwd, back = {"Z": lax.rem(Z + 1, 4)}, {"Z": lax.rem(Z + 3, 4)}
    sib = {"C": 1 - C}
    swapped = (C != H).astype(jnp.int32)

    count = {"s": 0, "r": 0}
    pending = []

    def sems(kind, n=1):
        first = count[kind]
        count[kind] += n
        return first

    def copy(src, dst, recv, dev):
        d = pltpu.make_async_remote_copy(
            src_ref=src, dst_ref=dst, send_sem=send_sem.at[sems("s")], recv_sem=recv_sem.at[recv],
            device_id=dev, device_id_type=MESH,
        )
        d.start()
        pending.append(d)

    def arrive(dst, recv):
        pltpu.make_async_remote_copy(
            src_ref=dst, dst_ref=dst, send_sem=send_sem.at[0], recv_sem=recv_sem.at[recv],
            device_id=sib, device_id_type=MESH,
        ).wait_recv()

    barrier = pltpu.get_barrier_semaphore()
    offsets = [(dh, dz) for dh in range(2) for dz in range(4) if dh + dz]
    peers = [{"H": lax.rem(H + dh, 2), "Z": lax.rem(Z + dz, 4)} for dh, dz in offsets]
    for dev in peers + [lo, cross, up, down, sib]:
        pl.semaphore_signal(barrier, inc=1, device_id=dev, device_id_type=MESH)

    @pl.when(C != H)
    def _():
        for b in range(2):
            pl.semaphore_signal(barrier, inc=1, device_id={"H": C, "L": b, "C": H}, device_id_type=MESH)

    pl.semaphore_wait(barrier, 12 + 2 * swapped)

    stat_r = sems("r", 7)
    for k, dev in enumerate(peers):
        copy(stats, statbuf.at[k], stat_r + k, dev)

    w1_r = sems("r", 2 * CHUNKS)

    def send_w1(j):
        copy(w1.at[j], w1buf.at[H, j], w1_r + j, lo)
        copy(w1.at[j], w1buf.at[H, j], w1_r + CHUNKS + j, cross)

    for k in range(7):
        arrive(statbuf.at[k], stat_r + k)
    summed = stats[...]
    for k in range(7):
        summed = summed + statbuf[k]
    column = jnp.transpose(jnp.concatenate([summed] * 16, axis=0))
    mean = column[:, 0:1] / width
    spread = column[:, 1:2] / width - mean * mean
    scale = lax.rsqrt(spread + EPS)
    normed[...] = ((tok[...].astype(F32) - mean) * scale * gain[...]).astype(BF16)

    x_r = sems("r", 2)
    x_s = sems("s", 2)

    def token_copy(b):
        return pltpu.make_async_remote_copy(
            src_ref=normed, dst_ref=xbuf.at[H, 0, L], send_sem=send_sem.at[x_s + b], recv_sem=recv_sem.at[x_r + L],
            device_id={"H": C, "L": b, "C": H}, device_id_type=MESH,
        )

    for b in range(2):
        mine = jnp.logical_and(C == H, L == b)

        @pl.when(mine)
        def _():
            xbuf[H, 0, b] = normed[...]

        @pl.when(jnp.logical_not(mine))
        def _():
            token_copy(b).start()

    for j in range(CHUNKS):
        send_w1(j)
    w2_r = sems("r", 8)
    for n, dev in enumerate((lo, cross)):
        for h in range(2):
            units = w_down.shape[0] // 2
            copy(w_attn.at[pl.ds(h * 128, 128)], w2buf.at[H, h, pl.ds(0, 128)], w2_r + 4 * n + 2 * h, dev)
            copy(w_down.at[pl.ds(h * units, units)], w2buf.at[H, h, pl.ds(128, units)], w2_r + 4 * n + 2 * h + 1, dev)

    yp_r, ym_r, ya_r, yb_r, sib_r = sems("r", 2), sems("r", 2), sems("r", 2), sems("r", 2), sems("r", 8)

    def to_sib(rel, b):
        copy(xbuf.at[C, rel, b], xbuf.at[C, rel, b], sib_r + 2 * rel + b, sib)

    for b in range(2):

        @pl.when(jnp.logical_not(jnp.logical_and(C == H, L == b)))
        def _():
            arrive(xbuf.at[C, 0, b], x_r + b)

        copy(xbuf.at[C, 0, b], xbuf.at[C, 3, b], yp_r + b, up)
        copy(xbuf.at[C, 0, b], xbuf.at[C, 1, b], ym_r + b, down)
        to_sib(0, b)
    for b in range(2):
        arrive(xbuf.at[C, 3, b], yp_r + b)
        copy(xbuf.at[C, 3, b, pl.ds(0, half)], xbuf.at[C, 2, b, pl.ds(0, half)], ya_r + b, up)
        to_sib(3, b)
        arrive(xbuf.at[C, 1, b], ym_r + b)
        copy(xbuf.at[C, 1, b, pl.ds(half, half)], xbuf.at[C, 2, b, pl.ds(half, half)], yb_r + b, down)
        to_sib(1, b)
    for b in range(2):
        arrive(xbuf.at[C, 2, b, pl.ds(0, half)], ya_r + b)
        arrive(xbuf.at[C, 2, b, pl.ds(half, half)], yb_r + b)
        to_sib(2, b)

    items = [(j, rel) for j in range(CHUNKS) for rel in RELS]
    n_items = len(items)
    r1a_r, r1b_r, r2p_r, r2m_r = (sems("r", n_items) for _ in range(4))
    dp_r, dm_r, da_r, db_r = (sems("r", 8) for _ in range(4))
    e_r = sems("r", 4)
    zp, zm, z2 = lax.rem(Z + 1, 4), lax.rem(Z + 3, 4), lax.rem(Z + 2, 4)
    seen_w, seen_x = set(), set()

    def s1(i):
        j, rel = items[i]
        if j not in seen_w:
            seen_w.add(j)
            arrive(w1buf.at[H, j], w1_r + j)
            arrive(w1buf.at[1 - H, j], w1_r + CHUNKS + j)
        if rel not in seen_x:
            seen_x.add(rel)
            for b in range(2):
                arrive(xbuf.at[1 - C, rel, b], sib_r + 2 * rel + b)

        @pl.loop(0, 4)
        def _(q):
            h, b = q // 2, q % 2
            acc = jnp.dot(xbuf[0, rel, b], w1buf[0, j, h], preferred_element_type=F32)
            acc = acc + jnp.dot(xbuf[1, rel, b], w1buf[1, j, h], preferred_element_type=F32)
            pbuf[i, q] = acc.astype(BF16)

        copy(pbuf.at[i, z2, pl.ds(0, half)], r1.at[0, i], r1a_r + i, fwd)
        copy(pbuf.at[i, z2, pl.ds(half, half)], r1.at[1, i], r1b_r + i, back)

    def s2(i):
        arrive(r1.at[0, i], r1a_r + i)
        pbuf[i, zp, pl.ds(0, half)] = (pbuf[i, zp, pl.ds(0, half)].astype(F32) + r1[0, i].astype(F32)).astype(BF16)
        copy(pbuf.at[i, zp], r2.at[0, i], r2p_r + i, fwd)
        arrive(r1.at[1, i], r1b_r + i)
        pbuf[i, zm, pl.ds(half, half)] = (
            pbuf[i, zm, pl.ds(half, half)].astype(F32) + r1[1, i].astype(F32)
        ).astype(BF16)
        copy(pbuf.at[i, zm], r2.at[1, i], r2m_r + i, back)

    def s3(i):
        j, rel = items[i]
        arrive(r2.at[0, i], r2p_r + i)
        arrive(r2.at[1, i], r2m_r + i)
        whole = (pbuf[i, Z].astype(F32) + r2[0, i].astype(F32) + r2[1, i].astype(F32)).astype(BF16)
        if j == 0:
            qkv[rel] = whole
            return
        if j == 1:
            both = qkv[rel].astype(F32)
            query = (head_norm(both[:, :HEAD_DIM]) * (1.0 / HEAD_DIM) ** 0.5).astype(BF16)
            keys = head_norm(both[:, HEAD_DIM:]).astype(BF16)
            scores = lax.dot_general(query, keys, (((1,), (1,)), ((), ())), preferred_element_type=F32)
            weights = jnp.exp(scores)
            probs = (weights / jnp.sum(weights, axis=-1, keepdims=True)).astype(BF16)
            mixed = jnp.dot(probs, whole[:, :HEAD_DIM], preferred_element_type=F32)
            hbuf[rel, Z, 0, :, pl.ds(0, HEAD_DIM)] = mixed.astype(BF16)
            hbuf[rel, Z, 0, :, pl.ds(HEAD_DIM, HEAD_DIM)] = gelu(whole[:, HEAD_DIM:].astype(F32)).astype(BF16)
        else:
            hbuf[rel, Z, 1] = gelu(whole.astype(F32)).astype(BF16)
        k = j - 1
        copy(hbuf.at[rel, Z, k], hbuf.at[rel, Z, k], dp_r + 2 * rel + k, fwd)
        copy(hbuf.at[rel, Z, k], hbuf.at[rel, Z, k], dm_r + 2 * rel + k, back)

    def relay(i):
        j, rel = items[i]
        if j == 0:
            return
        k = j - 1
        arrive(hbuf.at[rel, zm, k], dp_r + 2 * rel + k)
        top = hbuf.at[rel, zm, k, pl.ds(0, half)]
        copy(top, top, da_r + 2 * rel + k, fwd)
        arrive(hbuf.at[rel, zp, k], dm_r + 2 * rel + k)
        low = hbuf.at[rel, zp, k, pl.ds(half, half)]
        copy(low, low, db_r + 2 * rel + k, back)

    seen_w2 = []

    def e1(rel):
        if not seen_w2:
            seen_w2.append(1)
            units = w_down.shape[0] // 2
            for n, src in enumerate((H, 1 - H)):
                for h in range(2):
                    arrive(w2buf.at[src, h, pl.ds(0, 128)], w2_r + 4 * n + 2 * h)
                    arrive(w2buf.at[src, h, pl.ds(128, units)], w2_r + 4 * n + 2 * h + 1)
        for k in range(2):
            arrive(hbuf.at[rel, z2, k, pl.ds(0, half)], da_r + 2 * rel + k)
            arrive(hbuf.at[rel, z2, k, pl.ds(half, half)], db_r + 2 * rel + k)

        def product(f, b):
            acc = None
            for h in range(2):
                for k in range(2):
                    term = jnp.dot(
                        hbuf[rel, 2 * h + b, k], w2buf[f, h, pl.ds(k * 256, 256)], preferred_element_type=F32
                    )
                    acc = term if acc is None else acc + term
            return acc.astype(BF16)

        @pl.loop(0, 2)
        def _(b):
            osend[rel, b] = product(1 - C, b)

        copy(osend.at[rel], osib.at[rel], e_r + rel, sib)

        @pl.loop(0, 2)
        def _(b):
            obuf[rel, b] = product(C, b)

    ry_r = sems("r", 4)
    xr_r = sems("r", 2)
    xr_s = sems("s", 2)

    def final_copy(b):
        return pltpu.make_async_remote_copy(
            src_ref=xsend.at[b], dst_ref=xrecv.at[L], send_sem=send_sem.at[xr_s + b], recv_sem=recv_sem.at[xr_r + L],
            device_id={"H": C, "L": b, "C": H}, device_id_type=MESH,
        )

    def e2(rel):
        arrive(osib.at[rel], e_r + rel)
        for b in range(2):
            total = obuf[rel, b].astype(F32) + osib[rel, b].astype(F32)
            if rel == 1 and b == 0:
                arrive(ry1.at[0], ry_r)
                total = total + ry1[0].astype(F32)
            if rel == 3 and b == 1:
                arrive(ry1.at[1], ry_r + 1)
                total = total + ry1[1].astype(F32)
            if rel == 0:
                if b == 0:
                    arrive(ry2.at[0], ry_r + 2)
                    arrive(ry2.at[1], ry_r + 3)
                xsend[b] = (total + ry2[0, b].astype(F32) + ry2[1, b].astype(F32)).astype(BF16)
                mine = jnp.logical_and(C == H, L == b)

                @pl.when(mine)
                def _():
                    xrecv[b] = xsend[b]

                @pl.when(jnp.logical_not(mine))
                def _():
                    final_copy(b).start()
            else:
                obuf[rel, b] = total.astype(BF16)
        if rel == 2:
            copy(obuf.at[2, 0], ry1.at[0], ry_r, up)
            copy(obuf.at[2, 1], ry1.at[1], ry_r + 1, down)
        if rel == 1:
            copy(obuf.at[1], ry2.at[0], ry_r + 2, up)
        if rel == 3:
            copy(obuf.at[3], ry2.at[1], ry_r + 3, down)

    first_last = n_items - 4
    for t in range(n_items + 6):
        if t < n_items:
            s1(t)
        if 0 <= t - 1 < n_items:
            s2(t - 1)
        if 0 <= t - 2 < n_items:
            s3(t - 2)
        if 0 <= t - 3 < n_items:
            relay(t - 3)
        if first_last <= t - 4 < n_items:
            e1(items[t - 4][1])
        if first_last <= t - 5 < n_items:
            e2(items[t - 5][1])

    for b in range(2):

        @pl.when(jnp.logical_not(jnp.logical_and(C == H, L == b)))
        def _():
            arrive(xrecv.at[b], xr_r + b)

    out[...] = (tok[...].astype(F32) + xrecv[0].astype(F32) + xrecv[1].astype(F32)).astype(BF16)

    for d in pending:
        d.wait_send()
    for b in range(2):

        @pl.when(jnp.logical_not(jnp.logical_and(C == H, L == b)))
        def _():
            token_copy(b).wait_send()
            final_copy(b).wait_send()

    assert count["s"] <= N_SEND and count["r"] <= N_RECV, count


def local(tokens, norm_gain, w_qkv, w_up, w_attn_out, w_down):
    rows, feat = tokens.shape
    width = feat * lax.axis_size("H") * lax.axis_size("Z")
    tokens_f = tokens.astype(F32)
    sums = jnp.stack([jnp.sum(tokens_f, axis=1), jnp.sum(tokens_f * tokens_f, axis=1)])
    stats = jnp.concatenate([sums, jnp.zeros((6, rows), F32)], axis=0)
    units = w_up.shape[1] // 2
    by_head = jnp.concatenate(
        [
            w_qkv.reshape(feat, 3, 2, HEAD_DIM).transpose(2, 0, 1, 3).reshape(2, feat, 3 * HEAD_DIM),
            w_up.reshape(feat, 2, units).transpose(1, 0, 2),
        ],
        axis=2,
    )
    wide = by_head.shape[2] // CHUNKS
    w1 = by_head.reshape(2, feat, CHUNKS, wide).transpose(2, 0, 1, 3)
    n_items = 4 * CHUNKS
    half = rows // 2
    vmem = pltpu.VMEM
    scratch = [
        vmem((7, 8, rows), F32),
        vmem((rows, feat), BF16),
        vmem((2, 4, 2, rows, feat), BF16),
        vmem((2, CHUNKS, 2, feat, wide), BF16),
        vmem((2, 2, 512, feat), BF16),
        vmem((n_items, 4, rows, wide), BF16),
        vmem((2, n_items, half, wide), BF16),
        vmem((2, n_items, rows, wide), BF16),
        vmem((4, rows, wide), BF16),
        vmem((4, 4, 2, rows, 256), BF16),
        vmem((4, 2, rows, feat), BF16),
        vmem((4, 2, rows, feat), BF16),
        vmem((4, 2, rows, feat), BF16),
        vmem((2, rows, feat), BF16),
        vmem((2, 2, rows, feat), BF16),
        vmem((2, rows, feat), BF16),
        vmem((2, rows, feat), BF16),
        pltpu.SemaphoreType.DMA((N_SEND,)),
        pltpu.SemaphoreType.DMA((N_RECV,)),
    ]
    in_vmem = pl.BlockSpec(memory_space=pltpu.VMEM)
    anywhere = pl.BlockSpec(memory_space=pl.ANY)
    return pl.pallas_call(
        functools.partial(kernel, width),
        out_shape=jax.ShapeDtypeStruct((rows, feat), BF16),
        in_specs=[in_vmem] * 3 + [anywhere] * 3,
        out_specs=in_vmem,
        scratch_shapes=scratch,
        compiler_params=pltpu.CompilerParams(
            collective_id=0, has_side_effects=True, vmem_limit_bytes=60 * 1024 * 1024
        ),
        name="layer",
    )(tokens, stats, norm_gain[None, :], w1, w_attn_out, w_down)


def solution(mesh):
    torus = Mesh(mesh.devices.reshape(2, 4, 2, 2, 4), ("L", "Y", "C", "H", "Z"))
    in_specs = (P(DP, MP), P(MP), P(MP, None, DP), P(MP, DP), P(DP, MP), P(DP, MP))
    return jax.shard_map(local, mesh=torus, in_specs=in_specs, out_specs=P(DP, MP), check_vma=False)
```

time: 448 us -> 194 us (0.43)
  waiting for transfers between devices: 363 us -> 0 us
  Pallas kernels: 0 us -> 183 us
  matrix products: 26.7 us -> 0 us
  other arithmetic: 19.1 us -> 3.32 us
  blocking collectives: 14.7 us -> 0 us
  between operations: 13.3 us -> 0.05 us
    reduce_scatter x3 -> x0, waiting for transfers between devices: 213 us -> none  [the longest x1 151 us: local(): lax.psum_scatter(jnp.concatenate([jnp.dot(normed_all, w_heads, preferred_...]
    pallas_call x0 -> x1, Pallas kernels: none -> 183 us  [local(): pl.pallas_call(functools.partial(kernel, width), out_shape=jax.ShapeDtype...]
    all_gather x2 -> x0, waiting for transfers between devices: 150 us -> none  [the longest x1 110 us: local(): piece = lax.all_gather(hidden, 'mp', axis=0, tiled=True)]
    dot_general x6 -> x0, matrix products: 26.7 us -> none  [the longest x1 8.23 us: local(): jnp.dot(normed_all, w_heads, preferred_element_type=jnp.float32)]
    all_to_all x1 -> x0, blocking collectives: 14.7 us -> none  [sent_to_all(): lax.all_to_all(jnp.broadcast_to(array[None], (length, *array.shape)), axi...]
    concatenate x3 -> x2, other arithmetic: 12.3 us -> 2.09 us  [the longest x1 1.42 us: local(): jnp.concatenate([w_qkv.reshape(feat, 3, 2, HEAD_DIM).transpose(2, 0, 1, 3...]
  transfers between devices with their start and end apart: 5 -> 0, of which waited for: 5 -> 0; matrix products, arithmetic and copies ran while one was open for 0% -> 0% of each run, Pallas kernels for 0% -> 0%
where the time goes in v1:
time: 194 us
  Pallas kernels  183 us (94%)
  local copies, waits for them, and re-layouts  8.07 us (4%)
  other arithmetic  3.32 us (2%)
    pallas_call x1, Pallas kernels, local(): pl.pallas_call(functools.partial(kernel, width), out_shape=jax.ShapeDtype...  183 us
    unnamed x7, local copies, waits for them, and re-layouts  4.89 us

profile of v1, /device:TPU:1, one launch (start us, length us, event | category | flops | bytes accessed | tf_op | source)
XLA Modules:
  0.0 194.0 jit_solution(2812610750370466668)
XLA Ops:
  0.0 1.2 convert_reduce_fusion
  1.2 0.1 pad.4.clone
  1.3 0.7 maximum_maximum_fusion.stats
  2.0 0.0 copy-start
  2.0 1.7 copy.10
  3.7 0.1 copy.11
  3.7 0.0 copy-done
  3.7 1.4 copy.12
  5.2 1.4 pad_maximum_fusion
  6.6 0.0 copy-start.1
  6.6 2.4 %copy.13 = bf16[2,768,3,256]{3,1,0,2:T(8,128)(2,1)} copy(bf16[2,768,3,256]{1,3,2,0:T(8,128)(2,1)S(1)} %bitcast.12) | data formatting | bytes 4718592 | tf_op jit(solution)/shard_map/reshape | solution.py:369
  9.1 0.0 copy-done.1
  9.1 0.6 broadcast_in_dim.7.gain
  9.7 182.6 %layer.1 = bf16[256,768]{1,0:T(8,128)(2,1)} custom-call(bf16[256,768]{1,0:T(8,128)(2,1)} %tok.1, f32[8,256]{1,0:T(8,128)} %maximum_maximum_fusion.stats, f32[1,768]{1,0:T(1,128)} %broadcast_in_dim.7.gain, bf16[3,2,768,256]{3,2,1,0:T(8,128)(2,1)} %bitcast.11, bf16[256,768]{1,0:T(8,128)(2,1)} %w_attn.1, bf16[768,768]{1,0:T(8,128)(2,1)} %w_down.1), custom_call_target="tpu_custom_call" | custom-call | tf_op jit(solution)/shard_map/layer/pallas_call | solution.py:396
  192.3 1.8 copy.15
  (1 shorter events, 0.0 us)
Async XLA Ops:
  2.0 1.8 copy-start
  6.6 2.5 %copy-start.1 = (f32[768]{0:T(1024)S(1)}, f32[768]{0:T(1024)}, u32[]{:S(2)}) copy-start(f32[768]{0:T(1024)} %param.7) | copy-start | bytes 9220

commit v2 on v1

v2 whole, which is shorter than its diff:
```python
import functools

import jax
import jax.numpy as jnp
from jax import lax
from jax.experimental import pallas as pl
from jax.experimental.pallas import tpu as pltpu
from jax.sharding import Mesh
from jax.sharding import PartitionSpec as P

HEAD_DIM = 128
PATCHES = 256
EPS = 1e-06
MESH = pl.DeviceIdType.MESH
F32 = jnp.float32
BF16 = jnp.bfloat16
DP = ("L", "Y", "C")
MP = ("H", "Z")

CHUNKS = 6
WIDE = 2 * HEAD_DIM
PARTS = 3
ITEMS = (
    (0, 0), (1, 0), (0, 1), (0, 3), (1, 1), (1, 3), (2, 1), (2, 3), (0, 2), (1, 2), (2, 2), (3, 2), (3, 1), (4, 2),
    (5, 2), (4, 1), (5, 1), (3, 3), (4, 3), (5, 3), (2, 0), (3, 0), (4, 0), (5, 0),
)
LAGS = (2, 4, 6)
FAR_STEP = 8
OUT_STEPS = (
    (22, 1, 2, 0), (23, 2, 2, 0), (23, 1, 2, 1), (24, 2, 2, 1), (24, 1, 1, 0), (24, 1, 1, 1), (25, 2, 1, 0),
    (25, 1, 2, 2), (25, 1, 1, 2), (26, 2, 2, 2), (26, 2, 1, 1), (27, 1, 3, 0), (27, 1, 3, 1), (27, 1, 3, 2),
    (28, 2, 1, 2), (28, 2, 3, 0), (28, 2, 3, 1), (28, 2, 3, 2), (31, 1, 0, 0), (31, 1, 0, 1), (31, 2, 0, 0),
    (31, 1, 0, 2), (31, 2, 0, 1), (31, 2, 0, 2),
)
N_SEND = 224
N_RECV = 224


def gelu(u):
    return 0.5 * u * (1.0 + jnp.tanh(0.7978845608028654 * (u + 0.044715 * (u * u * u))))


def head_norm(values):
    mean = jnp.mean(values, axis=-1, keepdims=True)
    centered = values - mean
    spread = jnp.mean(centered * centered, axis=-1, keepdims=True)
    return centered * lax.rsqrt(spread + EPS)


def kernel(
    width,
    tok, gain, w_qkv, w_up, w_attn, w_down,
    out,
    stats, statbuf, xraw, xbuf, w1buf, w2buf, pbuf, r1, r2, qkv, hbuf, obuf, osend, osib, ry1, ry2, xsend, xrecv,
    send_sem, recv_sem,
):
    L, Y, C, H, Z = (lax.axis_index(a) for a in ("L", "Y", "C", "H", "Z"))
    rows, feat = tok.shape
    half = rows // 2
    near = ({"L": 1 - L, "H": C}, {"L": 1 - L, "H": 1 - C})
    up, down = {"Y": lax.rem(Y + 1, 4)}, {"Y": lax.rem(Y + 3, 4)}
    fwd, back = {"Z": lax.rem(Z + 1, 4)}, {"Z": lax.rem(Z + 3, 4)}
    sib = {"C": 1 - C}
    swapped = (C != H).astype(jnp.int32)
    straight = C == H

    count = {"s": 0, "r": 0}
    pending = []

    def sems(kind, n=1):
        first = count[kind]
        count[kind] += n
        return first

    def copy(src, dst, recv, dev):
        d = pltpu.make_async_remote_copy(
            src_ref=src, dst_ref=dst, send_sem=send_sem.at[sems("s")], recv_sem=recv_sem.at[recv],
            device_id=dev, device_id_type=MESH,
        )
        d.start()
        pending.append(d)

    def arrive(dst, recv):
        pltpu.make_async_remote_copy(
            src_ref=dst, dst_ref=dst, send_sem=send_sem.at[0], recv_sem=recv_sem.at[recv],
            device_id=sib, device_id_type=MESH,
        ).wait_recv()

    barrier = pltpu.get_barrier_semaphore()
    for dev in (*near, up, down, fwd, back, sib):
        pl.semaphore_signal(barrier, inc=1, device_id=dev, device_id_type=MESH)

    readers = [(dl, dz, dc) for dl in range(2) for dz in range(4) for dc in range(2)]

    def reader(dl, dz, dc):
        return {"H": C, "L": lax.rem(L + dl, 2), "Z": lax.rem(Z + dz, 4), "C": lax.rem(C + dc, 2)}

    def unless(condition, skip, f):
        if skip:
            pl.when(jnp.logical_not(condition))(f)
        else:
            f()

    for dh, dl, dz in [(dh, dl, dz) for dh in range(2) for dl in range(2) for dz in range(4)]:

        def greet():
            source = {"C": H, "H": lax.rem(H + dh, 2), "L": lax.rem(L + dl, 2), "Z": lax.rem(Z + dz, 4)}
            pl.semaphore_signal(barrier, inc=1, device_id=source, device_id_type=MESH)

        unless(straight, dh + dl + dz == 0, greet)

    w1_r = sems("r", 2 * CHUNKS)
    w2_r = sems("r", 2 * PARTS)

    def send_w1(j, dev):
        block = w_qkv.at[j] if j < 3 else w_up.at[:, pl.ds((j - 3) * WIDE, WIDE)]
        copy(block, w1buf.at[H, j], w1_r + H * CHUNKS + j, dev)

    def send_w2(f, dev):
        top, columns = w_attn.shape[0], pl.ds(f * WIDE, WIDE)
        copy(w_attn.at[:, columns], w2buf.at[H, f, pl.ds(0, top)], w2_r + H * PARTS + f, dev)
        copy(w_down.at[:, columns], w2buf.at[H, f, pl.ds(top, w_down.shape[0])], w2_r + H * PARTS + f, dev)

    tokens_f = tok[...].astype(F32)
    lane = lax.broadcasted_iota(jnp.int32, (rows, 128), 1)
    total = jnp.sum(tokens_f, axis=1, keepdims=True)
    squares = jnp.sum(tokens_f * tokens_f, axis=1, keepdims=True)
    stats[...] = jnp.transpose(jnp.where(lane == 0, total, jnp.where(lane == 1, squares, 0.0)))[0:8]
    for k in range(feat // rows):
        stats[pl.ds(2 + k, 1)] = gain[pl.ds(k * rows, rows)][None, :]

    pl.semaphore_wait(barrier, 23 - straight.astype(jnp.int32))

    stat_r = sems("r", 16)
    stat_s = sems("s", 16)

    def stat_copy(n):
        dl, dz, dc = readers[n]
        return pltpu.make_async_remote_copy(
            src_ref=stats, dst_ref=statbuf.at[H, dl, dz], send_sem=send_sem.at[stat_s + n],
            recv_sem=recv_sem.at[stat_r + 8 * H + 4 * dl + dz], device_id=reader(dl, dz, dc), device_id_type=MESH,
        )

    for n, r in enumerate(readers):
        unless(straight, r == (0, 0, 0), lambda: stat_copy(n).start())

    x_r = sems("r", 2)
    x_s = sems("s", 2)

    def token_copy(b):
        return pltpu.make_async_remote_copy(
            src_ref=tok, dst_ref=xraw.at[L], send_sem=send_sem.at[x_s + b], recv_sem=recv_sem.at[x_r + L],
            device_id={"H": C, "L": b, "C": H}, device_id_type=MESH,
        )

    for b in (1 - L, L):
        mine = jnp.logical_and(straight, L == b)

        @pl.when(jnp.logical_not(mine))
        def _():
            token_copy(b).start()

    send_w1(0, near[0])

    @pl.when(straight)
    def _():
        xraw[L] = tok[...]
        statbuf[H, 0, 0] = stats[...]

    yp_r, ym_r, ya_r, yb_r, sib_r = sems("r", 4), sems("r", 4), sems("r", 2), sems("r", 2), sems("r", 8)
    first, second = pl.ds(0, half), pl.ds(half, half)

    def to_sib(rel, b):
        copy(xbuf.at[C, rel, b], xbuf.at[C, rel, b], sib_r + 2 * rel + b, sib)

    early = lax.rem(L + swapped, 2)

    def start_y(b):
        mine = jnp.logical_and(straight, L == b)
        dl = lax.rem(L + b, 2)

        @pl.when(jnp.logical_not(mine))
        def _():
            arrive(statbuf.at[H, dl, 0], stat_r + 8 * H + 4 * dl)

        arrive(statbuf.at[1 - H, dl, 0], stat_r + 8 * (1 - H) + 4 * dl)
        for src in range(2):
            for dz in range(1, 4):
                arrive(statbuf.at[src, dl, dz], stat_r + 8 * src + 4 * dl + dz)
        summed = statbuf[0, dl, 0]
        for src, dz in [(0, 1), (0, 2), (0, 3), (1, 0), (1, 1), (1, 2), (1, 3)]:
            summed = summed + statbuf[src, dl, dz]
        column = jnp.transpose(jnp.concatenate([summed] * 16, axis=0))
        mean = column[:, 0:1] / width
        spread = column[:, 1:2] / width - mean * mean
        scale = lax.rsqrt(spread + EPS)
        gains = jnp.concatenate([statbuf[C, dl, 0, pl.ds(2 + k, 1)] for k in range(feat // rows)], axis=1)

        @pl.when(jnp.logical_not(mine))
        def _():
            arrive(xraw.at[b], x_r + b)

        xbuf[C, 0, b] = ((xraw[b].astype(F32) - mean) * scale * gains).astype(BF16)
        copy(xbuf.at[C, 0, b, first], xbuf.at[C, 3, b, first], yp_r + 2 * b, up)
        copy(xbuf.at[C, 0, b, second], xbuf.at[C, 1, b, second], ym_r + 2 * b + 1, down)
        copy(xbuf.at[C, 0, b, second], xbuf.at[C, 3, b, second], yp_r + 2 * b + 1, up)
        copy(xbuf.at[C, 0, b, first], xbuf.at[C, 1, b, first], ym_r + 2 * b, down)
        to_sib(0, b)

    def relay_y(b):
        arrive(xbuf.at[C, 3, b, first], yp_r + 2 * b)
        copy(xbuf.at[C, 3, b, first], xbuf.at[C, 2, b, first], ya_r + b, up)
        arrive(xbuf.at[C, 1, b, second], ym_r + 2 * b + 1)
        copy(xbuf.at[C, 1, b, second], xbuf.at[C, 2, b, second], yb_r + b, down)
        arrive(xbuf.at[C, 3, b, second], yp_r + 2 * b + 1)
        to_sib(3, b)
        arrive(xbuf.at[C, 1, b, first], ym_r + 2 * b)
        to_sib(1, b)

    def far_y(b):
        arrive(xbuf.at[C, 2, b, first], ya_r + b)
        arrive(xbuf.at[C, 2, b, second], yb_r + b)
        to_sib(2, b)

    start_y(early)
    start_y(1 - early)
    send_w1(0, near[1])
    for j in range(1, CHUNKS):
        for dev in near:
            send_w1(j, dev)
    for f in range(PARTS):
        for dev in near:
            send_w2(f, dev)

    items = ITEMS
    n_items = len(items)
    r1a_r, r1b_r, r2p_r, r2m_r = (sems("r", n_items) for _ in range(4))
    dp_r, dm_r, da_r, db_r = (sems("r", 8) for _ in range(4))
    e_r = sems("r", 4 * PARTS)
    zp, zm, z2 = lax.rem(Z + 1, 4), lax.rem(Z + 3, 4), lax.rem(Z + 2, 4)
    seen_w, seen_x = set(), set()

    def s1(i):
        j, rel = items[i]
        if j not in seen_w:
            seen_w.add(j)
            for src in range(2):
                arrive(w1buf.at[src, j], w1_r + src * CHUNKS + j)
        if rel not in seen_x:
            seen_x.add(rel)
            for b in range(2):
                arrive(xbuf.at[1 - C, rel, b], sib_r + 2 * rel + b)

        @pl.loop(0, 2)
        def _(b):
            acc = jnp.dot(xbuf[0, rel, b], w1buf[0, j], preferred_element_type=F32)
            acc = acc + jnp.dot(xbuf[1, rel, b], w1buf[1, j], preferred_element_type=F32)
            pbuf[i, b] = acc[:, :HEAD_DIM].astype(BF16)
            pbuf[i, 2 + b] = acc[:, HEAD_DIM:].astype(BF16)

        copy(pbuf.at[i, z2, pl.ds(0, half)], r1.at[0, i], r1a_r + i, fwd)
        copy(pbuf.at[i, z2, pl.ds(half, half)], r1.at[1, i], r1b_r + i, back)

    def s2(i):
        arrive(r1.at[0, i], r1a_r + i)
        pbuf[i, zp, pl.ds(0, half)] = (pbuf[i, zp, pl.ds(0, half)].astype(F32) + r1[0, i].astype(F32)).astype(BF16)
        copy(pbuf.at[i, zp], r2.at[0, i], r2p_r + i, fwd)
        arrive(r1.at[1, i], r1b_r + i)
        pbuf[i, zm, pl.ds(half, half)] = (
            pbuf[i, zm, pl.ds(half, half)].astype(F32) + r1[1, i].astype(F32)
        ).astype(BF16)
        copy(pbuf.at[i, zm], r2.at[1, i], r2m_r + i, back)

    def s3(i):
        j, rel = items[i]
        arrive(r2.at[0, i], r2p_r + i)
        arrive(r2.at[1, i], r2m_r + i)
        whole = (pbuf[i, Z].astype(F32) + r2[0, i].astype(F32) + r2[1, i].astype(F32)).astype(BF16)
        if j < 3:
            qkv[rel, j] = whole
        if j == 2:
            query = (head_norm(qkv[rel, 0].astype(F32)) * (1.0 / HEAD_DIM) ** 0.5).astype(BF16)
            keys = head_norm(qkv[rel, 1].astype(F32)).astype(BF16)
            scores = lax.dot_general(query, keys, (((1,), (1,)), ((), ())), preferred_element_type=F32)
            weights = jnp.exp(scores)
            probs = (weights / jnp.sum(weights, axis=-1, keepdims=True)).astype(BF16)
            hbuf[rel, Z, 0] = jnp.dot(probs, whole, preferred_element_type=F32).astype(BF16)
        if j >= 3:
            hbuf[rel, Z, j - 2] = gelu(whole.astype(F32)).astype(BF16)
        if j in (3, 5):
            k = (j - 3) // 2
            mine = hbuf.at[rel, Z, pl.ds(2 * k, 2)]
            copy(mine, mine, dp_r + 2 * rel + k, fwd)
            copy(mine, mine, dm_r + 2 * rel + k, back)

    def relay(i):
        j, rel = items[i]
        if j not in (3, 5):
            return
        k = (j - 3) // 2
        arrive(hbuf.at[rel, zm, pl.ds(2 * k, 2)], dp_r + 2 * rel + k)
        top = hbuf.at[rel, zm, pl.ds(2 * k, 2), pl.ds(0, half)]
        copy(top, top, da_r + 2 * rel + k, fwd)
        arrive(hbuf.at[rel, zp, pl.ds(2 * k, 2)], dm_r + 2 * rel + k)
        low = hbuf.at[rel, zp, pl.ds(2 * k, 2), pl.ds(half, half)]
        copy(low, low, db_r + 2 * rel + k, back)

    seen_w2, seen_h = set(), set()

    def e1(rel, f):
        if f not in seen_w2:
            seen_w2.add(f)
            for src in range(2):
                arrive(w2buf.at[src, f], w2_r + src * PARTS + f)
        if rel not in seen_h:
            seen_h.add(rel)
            for k in range(2):
                arrive(hbuf.at[rel, z2, pl.ds(2 * k, 2), pl.ds(0, half)], da_r + 2 * rel + k)
                arrive(hbuf.at[rel, z2, pl.ds(2 * k, 2), pl.ds(half, half)], db_r + 2 * rel + k)

        def product(side, b):
            hidden = jnp.concatenate([hbuf[rel, 2 * h + b, k] for k in range(4) for h in range(2)], axis=1)
            return jnp.dot(hidden, w2buf[side, f], preferred_element_type=F32).astype(BF16)

        @pl.loop(0, 2)
        def _(b):
            osend[rel, f, b] = product(1 - C, b)

        copy(osend.at[rel, f], osib.at[rel, f], e_r + rel * PARTS + f, sib)

        @pl.loop(0, 2)
        def _(b):
            obuf[rel, f, b] = product(C, b)

    ry_r = sems("r", 4 * PARTS)
    xr_r = sems("r", 2 * PARTS)
    xr_s = sems("s", 2 * PARTS)

    def final_copy(b, f):
        return pltpu.make_async_remote_copy(
            src_ref=xsend.at[f, b], dst_ref=xrecv.at[f, L], send_sem=send_sem.at[xr_s + 2 * f + b],
            recv_sem=recv_sem.at[xr_r + 2 * f + L], device_id={"H": C, "L": b, "C": H}, device_id_type=MESH,
        )

    def e2(rel, f):
        arrive(osib.at[rel, f], e_r + rel * PARTS + f)
        ry = ry_r + 4 * f
        for b in range(2):
            total = obuf[rel, f, b].astype(F32) + osib[rel, f, b].astype(F32)
            if rel == 1 and b == 0:
                arrive(ry1.at[f, 0], ry)
                total = total + ry1[f, 0].astype(F32)
            if rel == 3 and b == 1:
                arrive(ry1.at[f, 1], ry + 1)
                total = total + ry1[f, 1].astype(F32)
            if rel == 0:
                if b == 0:
                    arrive(ry2.at[f, 0], ry + 2)
                    arrive(ry2.at[f, 1], ry + 3)
                xsend[f, b] = (total + ry2[f, 0, b].astype(F32) + ry2[f, 1, b].astype(F32)).astype(BF16)
                mine = jnp.logical_and(C == H, L == b)

                @pl.when(mine)
                def _():
                    xrecv[f, b] = xsend[f, b]

                @pl.when(jnp.logical_not(mine))
                def _():
                    final_copy(b, f).start()
            else:
                obuf[rel, f, b] = total.astype(BF16)
        if rel == 2:
            copy(obuf.at[2, f, 0], ry1.at[f, 0], ry, up)
            copy(obuf.at[2, f, 1], ry1.at[f, 1], ry + 1, down)
        if rel == 1:
            copy(obuf.at[1, f], ry2.at[f, 0], ry + 2, up)
        if rel == 3:
            copy(obuf.at[3, f], ry2.at[f, 1], ry + 3, down)

    for t in range(max(n_items + LAGS[2], OUT_STEPS[-1][0] + 1)):
        if t == 0:
            relay_y(early)
        if t == 2:
            relay_y(1 - early)
        if t == FAR_STEP:
            far_y(early)
            far_y(1 - early)
        for lag, stage in zip((0, *LAGS), (s1, s2, s3, relay)):
            if 0 <= t - lag < n_items:
                stage(t - lag)
        for step, stage, rel, f in OUT_STEPS:
            if step == t and stage == 1:
                e1(rel, f)
            if step == t and stage == 2:
                e2(rel, f)

    for f in range(PARTS):
        for b in range(2):

            @pl.when(jnp.logical_not(jnp.logical_and(C == H, L == b)))
            def _():
                arrive(xrecv.at[f, b], xr_r + 2 * f + b)

        columns = pl.ds(f * WIDE, WIDE)
        out[:, columns] = (
            tok[:, columns].astype(F32) + xrecv[f, 0].astype(F32) + xrecv[f, 1].astype(F32)
        ).astype(BF16)

    for n, r in enumerate(readers):
        unless(straight, r == (0, 0, 0), lambda: stat_copy(n).wait_send())
    for d in pending:
        d.wait_send()
    for b in range(2):

        @pl.when(jnp.logical_not(jnp.logical_and(C == H, L == b)))
        def _():
            token_copy(b).wait_send()

        @pl.when(jnp.logical_not(jnp.logical_and(C == H, L == b)))
        def _():
            for f in range(PARTS):
                final_copy(b, f).wait_send()

    assert count["s"] <= N_SEND and count["r"] <= N_RECV, count


def local(tokens, norm_gain, w_qkv, w_up, w_attn_out, w_down):
    rows, feat = tokens.shape
    width = feat * lax.axis_size("H") * lax.axis_size("Z")
    n_items = len(ITEMS)
    half = rows // 2
    vmem = pltpu.VMEM
    out_part = (PARTS, 2, rows, WIDE)
    scratch = [
        vmem((8, rows), F32),
        vmem((2, 2, 4, 8, rows), F32),
        vmem((2, rows, feat), BF16),
        vmem((2, 4, 2, rows, feat), BF16),
        vmem((2, CHUNKS, feat, WIDE), BF16),
        vmem((2, PARTS, w_attn_out.shape[0] + w_down.shape[0], WIDE), BF16),
        vmem((n_items, 4, rows, HEAD_DIM), BF16),
        vmem((2, n_items, half, HEAD_DIM), BF16),
        vmem((2, n_items, rows, HEAD_DIM), BF16),
        vmem((4, 3, rows, HEAD_DIM), BF16),
        vmem((4, 4, 4, rows, HEAD_DIM), BF16),
        vmem((4, *out_part), BF16),
        vmem((4, *out_part), BF16),
        vmem((4, *out_part), BF16),
        vmem((PARTS, 2, rows, WIDE), BF16),
        vmem((PARTS, 2, 2, rows, WIDE), BF16),
        vmem(out_part, BF16),
        vmem(out_part, BF16),
        pltpu.SemaphoreType.DMA((N_SEND,)),
        pltpu.SemaphoreType.DMA((N_RECV,)),
    ]
    in_vmem = pl.BlockSpec(memory_space=pltpu.VMEM)
    anywhere = pl.BlockSpec(memory_space=pl.ANY)
    return pl.pallas_call(
        functools.partial(kernel, width),
        out_shape=jax.ShapeDtypeStruct((rows, feat), BF16),
        in_specs=[in_vmem] * 2 + [anywhere] * 4,
        out_specs=in_vmem,
        scratch_shapes=scratch,
        compiler_params=pltpu.CompilerParams(
            collective_id=0, has_side_effects=True, vmem_limit_bytes=60 * 1024 * 1024
        ),
        name="layer",
    )(tokens, norm_gain, w_qkv.transpose(1, 0, 2), w_up, w_attn_out, w_down)


def solution(mesh):
    torus = Mesh(mesh.devices.reshape(2, 4, 2, 2, 4), ("L", "Y", "C", "H", "Z"))
    in_specs = (P(DP, MP), P(MP), P(MP, None, DP), P(MP, DP), P(DP, MP), P(DP, MP))
    return jax.shard_map(local, mesh=torus, in_specs=in_specs, out_specs=P(DP, MP), check_vma=False)
```

time: 194 us -> 162 us (0.84)
  Pallas kernels: 183 us -> 160 us
  local copies, waits for them, and re-layouts: 8.07 us -> 1.77 us
  other arithmetic: 3.32 us -> 0 us
    pallas_call x1, Pallas kernels: 183 us -> 160 us  [local(): pl.pallas_call(functools.partial(kernel, width), out_shape=jax.ShapeDtype...]
    unnamed x7 -> x1, local copies, waits for them, and re-layouts: 4.89 us -> 1.77 us
    reshape x1 -> x0, local copies, waits for them, and re-layouts: 2.44 us -> none  [local(): w1 = by_head.reshape(2, feat, CHUNKS, wide).transpose(2, 0, 1, 3)]
    concatenate x2 -> x0, other arithmetic: 2.09 us -> none  [the longest x1 1.42 us: local(): jnp.concatenate([w_qkv.reshape(feat, 3, 2, HEAD_DIM).transpose(2, 0, 1, 3...]
where the time goes in v2:
time: 162 us
  Pallas kernels  160 us (99%)
  local copies, waits for them, and re-layouts  1.77 us (1%)
    pallas_call x1, Pallas kernels, local(): pl.pallas_call(functools.partial(kernel, width), out_shape=jax.ShapeDtype...  160 us

profile of v2, /device:TPU:1, one launch (start us, length us, event | category | flops | bytes accessed | tf_op | source)
XLA Modules:
  0.0 161.7 jit_solution(5855688318350446540)
XLA Ops:
  0.0 159.9 %layer.1 = bf16[256,768]{1,0:T(8,128)(2,1)} custom-call(bf16[256,768]{1,0:T(8,128)(2,1)} %tok.1, f32[768]{0:T(1024)} %gain.1, bf16[3,768,256]{2,1,0:T(8,128)(2,1)} %bitcast.1, bf16[768,768]{1,0:T(8,128)(2,1)} %w_up.1, bf16[256,768]{1,0:T(8,128)(2,1)} %w_attn.1, bf16[768,768]{1,0:T(8,128)(2,1)} %w_down.1), custom_call_target="tpu_custom_call" | custom-call | tf_op jit(solution)/shard_map/layer/pallas_call | solution.py:458
  159.9 1.8 %copy.8 = bf16[256,768]{1,0:T(8,128)(2,1)} copy(bf16[256,768]{1,0:T(8,128)(2,1)} %layer.1) | data formatting | bytes 786432

commit v3 on v2

--- a/solution.py
+++ b/solution.py
@@ -20,17 +20,21 @@
 CHUNKS = 6
 WIDE = 2 * HEAD_DIM
 PARTS = 3
-ITEMS = (
-    (0, 0), (1, 0), (0, 1), (0, 3), (1, 1), (1, 3), (2, 1), (2, 3), (0, 2), (1, 2), (2, 2), (3, 2), (3, 1), (4, 2),
-    (5, 2), (4, 1), (5, 1), (3, 3), (4, 3), (5, 3), (2, 0), (3, 0), (4, 0), (5, 0),
-)
-LAGS = (2, 4, 6)
-FAR_STEP = 8
-OUT_STEPS = (
-    (22, 1, 2, 0), (23, 2, 2, 0), (23, 1, 2, 1), (24, 2, 2, 1), (24, 1, 1, 0), (24, 1, 1, 1), (25, 2, 1, 0),
-    (25, 1, 2, 2), (25, 1, 1, 2), (26, 2, 2, 2), (26, 2, 1, 1), (27, 1, 3, 0), (27, 1, 3, 1), (27, 1, 3, 2),
-    (28, 2, 1, 2), (28, 2, 3, 0), (28, 2, 3, 1), (28, 2, 3, 2), (31, 1, 0, 0), (31, 1, 0, 1), (31, 2, 0, 0),
-    (31, 1, 0, 2), (31, 2, 0, 1), (31, 2, 0, 2),
+ORDER = (
+    ("y1", 0, 0), ("s1", 0, 0), ("y2", 0, 0), ("s2", 0, 0), ("s3", 0, 0), ("s1", 1, 0), ("s1", 0, 1), ("s1", 1, 1),
+    ("s1", 0, 3), ("s1", 1, 3), ("s2", 1, 0), ("s2", 0, 1), ("s2", 1, 1), ("y3", 0, 0), ("s2", 0, 3), ("s2", 1, 3),
+    ("s3", 1, 0), ("s3", 0, 1), ("s1", 2, 1), ("s3", 1, 1), ("s1", 0, 2), ("s3", 0, 3), ("s1", 1, 2), ("s1", 2, 2),
+    ("s3", 1, 3), ("s1", 2, 3), ("s2", 2, 1), ("s2", 0, 2), ("s2", 1, 2), ("s2", 2, 2), ("s2", 2, 3), ("s3", 2, 1),
+    ("s3", 0, 2), ("s1", 3, 1), ("s3", 1, 2), ("s1", 3, 2), ("s3", 2, 2), ("s1", 3, 3), ("s3", 2, 3), ("s2", 3, 1),
+    ("s1", 4, 1), ("s2", 3, 2), ("s2", 3, 3), ("s3", 3, 1), ("s2", 4, 1), ("s3", 3, 2), ("s3", 3, 3), ("s4", 0, 1),
+    ("s3", 4, 1), ("s4", 0, 2), ("s1", 5, 1), ("s4", 0, 3), ("s1", 4, 2), ("s1", 5, 2), ("s2", 5, 1), ("s1", 4, 3),
+    ("s2", 4, 2), ("s2", 5, 2), ("s3", 5, 1), ("s2", 4, 3), ("s3", 4, 2), ("s3", 5, 2), ("s4", 1, 1), ("s3", 4, 3),
+    ("s1", 2, 0), ("s1", 5, 3), ("s4", 1, 2), ("e1", 0, 1), ("e1", 1, 1), ("s2", 2, 0), ("s2", 5, 3), ("e1", 0, 2),
+    ("e1", 2, 1), ("e1", 1, 2), ("e2", 0, 2), ("s3", 2, 0), ("s3", 5, 3), ("e1", 2, 2), ("e2", 1, 2), ("s1", 3, 0),
+    ("e2", 2, 2), ("s1", 4, 0), ("s1", 5, 0), ("e2", 0, 1), ("s4", 1, 3), ("s2", 3, 0), ("s2", 4, 0), ("e2", 1, 1),
+    ("s2", 5, 0), ("e1", 0, 3), ("e2", 2, 1), ("s3", 3, 0), ("e1", 1, 3), ("s3", 4, 0), ("e2", 0, 3), ("e1", 2, 3),
+    ("s3", 5, 0), ("e2", 1, 3), ("e2", 2, 3), ("s4", 0, 0), ("s4", 1, 0), ("e1", 0, 0), ("e1", 1, 0), ("e1", 2, 0),
+    ("e2", 0, 0), ("e2", 1, 0), ("e2", 2, 0),
 )
 N_SEND = 224
 N_RECV = 224
@@ -144,13 +148,16 @@
     for n, r in enumerate(readers):
         unless(straight, r == (0, 0, 0), lambda: stat_copy(n).start())
 
-    x_r = sems("r", 2)
-    x_s = sems("s", 2)
-
-    def token_copy(b):
+    x_r = sems("r", 4)
+    x_s = sems("s", 4)
+
+    first, second = pl.ds(0, half), pl.ds(half, half)
+    halves = (first, second)
+
+    def token_copy(b, n):
         return pltpu.make_async_remote_copy(
-            src_ref=tok, dst_ref=xraw.at[L], send_sem=send_sem.at[x_s + b], recv_sem=recv_sem.at[x_r + L],
-            device_id={"H": C, "L": b, "C": H}, device_id_type=MESH,
+            src_ref=tok.at[halves[n]], dst_ref=xraw.at[L, halves[n]], send_sem=send_sem.at[x_s + 2 * b + n],
+            recv_sem=recv_sem.at[x_r + 2 * L + n], device_id={"H": C, "L": b, "C": H}, device_id_type=MESH,
         )
 
     for b in (1 - L, L):
@@ -158,7 +165,8 @@
 
         @pl.when(jnp.logical_not(mine))
         def _():
-            token_copy(b).start()
+            for n in range(2):
+                token_copy(b, n).start()
 
     send_w1(0, near[0])
 
@@ -168,7 +176,6 @@
         statbuf[H, 0, 0] = stats[...]
 
     yp_r, ym_r, ya_r, yb_r, sib_r = sems("r", 4), sems("r", 4), sems("r", 2), sems("r", 2), sems("r", 8)
-    first, second = pl.ds(0, half), pl.ds(half, half)
 
     def to_sib(rel, b):
         copy(xbuf.at[C, rel, b], xbuf.at[C, rel, b], sib_r + 2 * rel + b, sib)
@@ -196,26 +203,27 @@
         scale = lax.rsqrt(spread + EPS)
         gains = jnp.concatenate([statbuf[C, dl, 0, pl.ds(2 + k, 1)] for k in range(feat // rows)], axis=1)
 
-        @pl.when(jnp.logical_not(mine))
-        def _():
-            arrive(xraw.at[b], x_r + b)
-
-        xbuf[C, 0, b] = ((xraw[b].astype(F32) - mean) * scale * gains).astype(BF16)
-        copy(xbuf.at[C, 0, b, first], xbuf.at[C, 3, b, first], yp_r + 2 * b, up)
-        copy(xbuf.at[C, 0, b, second], xbuf.at[C, 1, b, second], ym_r + 2 * b + 1, down)
-        copy(xbuf.at[C, 0, b, second], xbuf.at[C, 3, b, second], yp_r + 2 * b + 1, up)
-        copy(xbuf.at[C, 0, b, first], xbuf.at[C, 1, b, first], ym_r + 2 * b, down)
+        for n, part in enumerate(halves):
+
+            @pl.when(jnp.logical_not(mine))
+            def _():
+                arrive(xraw.at[b, part], x_r + 2 * b + n)
+
+            at = slice(n * half, (n + 1) * half)
+            xbuf[C, 0, b, part] = ((xraw[b, part].astype(F32) - mean[at]) * scale[at] * gains).astype(BF16)
+            copy(xbuf.at[C, 0, b, part], xbuf.at[C, 3, b, part], yp_r + 2 * b + n, up)
+            copy(xbuf.at[C, 0, b, part], xbuf.at[C, 1, b, part], ym_r + 2 * b + n, down)
         to_sib(0, b)
 
     def relay_y(b):
         arrive(xbuf.at[C, 3, b, first], yp_r + 2 * b)
         copy(xbuf.at[C, 3, b, first], xbuf.at[C, 2, b, first], ya_r + b, up)
+        arrive(xbuf.at[C, 1, b, first], ym_r + 2 * b)
         arrive(xbuf.at[C, 1, b, second], ym_r + 2 * b + 1)
         copy(xbuf.at[C, 1, b, second], xbuf.at[C, 2, b, second], yb_r + b, down)
+        to_sib(1, b)
         arrive(xbuf.at[C, 3, b, second], yp_r + 2 * b + 1)
         to_sib(3, b)
-        arrive(xbuf.at[C, 1, b, first], ym_r + 2 * b)
-        to_sib(1, b)
 
     def far_y(b):
         arrive(xbuf.at[C, 2, b, first], ya_r + b)
@@ -232,16 +240,15 @@
         for dev in near:
             send_w2(f, dev)
 
-    items = ITEMS
-    n_items = len(items)
+    n_items = 4 * CHUNKS
     r1a_r, r1b_r, r2p_r, r2m_r = (sems("r", n_items) for _ in range(4))
     dp_r, dm_r, da_r, db_r = (sems("r", 8) for _ in range(4))
     e_r = sems("r", 4 * PARTS)
     zp, zm, z2 = lax.rem(Z + 1, 4), lax.rem(Z + 3, 4), lax.rem(Z + 2, 4)
     seen_w, seen_x = set(), set()
 
-    def s1(i):
-        j, rel = items[i]
+    def s1(j, rel):
+        i = 4 * j + rel
         if j not in seen_w:
             seen_w.add(j)
             for src in range(2):
@@ -261,7 +268,8 @@
         copy(pbuf.at[i, z2, pl.ds(0, half)], r1.at[0, i], r1a_r + i, fwd)
         copy(pbuf.at[i, z2, pl.ds(half, half)], r1.at[1, i], r1b_r + i, back)
 
-    def s2(i):
+    def s2(j, rel):
+        i = 4 * j + rel
         arrive(r1.at[0, i], r1a_r + i)
         pbuf[i, zp, pl.ds(0, half)] = (pbuf[i, zp, pl.ds(0, half)].astype(F32) + r1[0, i].astype(F32)).astype(BF16)
         copy(pbuf.at[i, zp], r2.at[0, i], r2p_r + i, fwd)
@@ -271,8 +279,8 @@
         ).astype(BF16)
         copy(pbuf.at[i, zm], r2.at[1, i], r2m_r + i, back)
 
-    def s3(i):
-        j, rel = items[i]
+    def s3(j, rel):
+        i = 4 * j + rel
         arrive(r2.at[0, i], r2p_r + i)
         arrive(r2.at[1, i], r2m_r + i)
         whole = (pbuf[i, Z].astype(F32) + r2[0, i].astype(F32) + r2[1, i].astype(F32)).astype(BF16)
@@ -293,11 +301,7 @@
             copy(mine, mine, dp_r + 2 * rel + k, fwd)
             copy(mine, mine, dm_r + 2 * rel + k, back)
 
-    def relay(i):
-        j, rel = items[i]
-        if j not in (3, 5):
-            return
-        k = (j - 3) // 2
+    def relay(k, rel):
         arrive(hbuf.at[rel, zm, pl.ds(2 * k, 2)], dp_r + 2 * rel + k)
         top = hbuf.at[rel, zm, pl.ds(2 * k, 2), pl.ds(0, half)]
         copy(top, top, da_r + 2 * rel + k, fwd)
@@ -307,7 +311,7 @@
 
     seen_w2, seen_h = set(), set()
 
-    def e1(rel, f):
+    def e1(f, rel):
         if f not in seen_w2:
             seen_w2.add(f)
             for src in range(2):
@@ -342,7 +346,7 @@
             recv_sem=recv_sem.at[xr_r + 2 * f + L], device_id={"H": C, "L": b, "C": H}, device_id_type=MESH,
         )
 
-    def e2(rel, f):
+    def e2(f, rel):
         arrive(osib.at[rel, f], e_r + rel * PARTS + f)
         ry = ry_r + 4 * f
         for b in range(2):
@@ -377,22 +381,14 @@
         if rel == 3:
             copy(obuf.at[3, f], ry2.at[f, 1], ry + 3, down)
 
-    for t in range(max(n_items + LAGS[2], OUT_STEPS[-1][0] + 1)):
-        if t == 0:
-            relay_y(early)
-        if t == 2:
-            relay_y(1 - early)
-        if t == FAR_STEP:
-            far_y(early)
-            far_y(1 - early)
-        for lag, stage in zip((0, *LAGS), (s1, s2, s3, relay)):
-            if 0 <= t - lag < n_items:
-                stage(t - lag)
-        for step, stage, rel, f in OUT_STEPS:
-            if step == t and stage == 1:
-                e1(rel, f)
-            if step == t and stage == 2:
-                e2(rel, f)
+    stages = {
+        "y1": lambda a, rel: relay_y(early),
+        "y2": lambda a, rel: relay_y(1 - early),
+        "y3": lambda a, rel: (far_y(early), far_y(1 - early)),
+        "s1": s1, "s2": s2, "s3": s3, "s4": relay, "e1": e1, "e2": e2,
+    }
+    for stage, a, rel in ORDER:
+        stages[stage](a, rel)
 
     for f in range(PARTS):
         for b in range(2):
@@ -414,7 +410,8 @@
 
         @pl.when(jnp.logical_not(jnp.logical_and(C == H, L == b)))
         def _():
-            token_copy(b).wait_send()
+            for n in range(2):
+                token_copy(b, n).wait_send()
 
         @pl.when(jnp.logical_not(jnp.logical_and(C == H, L == b)))
         def _():
@@ -427,7 +424,7 @@
 def local(tokens, norm_gain, w_qkv, w_up, w_attn_out, w_down):
     rows, feat = tokens.shape
     width = feat * lax.axis_size("H") * lax.axis_size("Z")
-    n_items = len(ITEMS)
+    n_items = 4 * CHUNKS
     half = rows // 2
     vmem = pltpu.VMEM
     out_part = (PARTS, 2, rows, WIDE)

time: 162 us -> 155 us (0.957)
  Pallas kernels: 160 us -> 153 us
    pallas_call x1, Pallas kernels: 160 us -> 153 us  [local(): pl.pallas_call(functools.partial(kernel, width), out_shape=jax.ShapeDtype...]
where the time goes in v3:
time: 155 us
  Pallas kernels  153 us (99%)
  local copies, waits for them, and re-layouts  1.77 us (1%)
    pallas_call x1, Pallas kernels, local(): pl.pallas_call(functools.partial(kernel, width), out_shape=jax.ShapeDtype...  153 us

profile of v3, /device:TPU:1, one launch (start us, length us, event | category | flops | bytes accessed | tf_op | source)
XLA Modules:
  0.0 155.1 jit_solution(14737402305276868954)
XLA Ops:
  0.0 153.3 %layer.1 = bf16[256,768]{1,0:T(8,128)(2,1)} custom-call(bf16[256,768]{1,0:T(8,128)(2,1)} %tok.1, f32[768]{0:T(1024)} %gain.1, bf16[3,768,256]{2,1,0:T(8,128)(2,1)} %bitcast.1, bf16[768,768]{1,0:T(8,128)(2,1)} %w_up.1, bf16[256,768]{1,0:T(8,128)(2,1)} %w_attn.1, bf16[768,768]{1,0:T(8,128)(2,1)} %w_down.1), custom_call_target="tpu_custom_call" | custom-call | tf_op jit(solution)/shard_map/layer/pallas_call | solution.py:455
  153.3 1.8 %copy.8 = bf16[256,768]{1,0:T(8,128)(2,1)} copy(bf16[256,768]{1,0:T(8,128)(2,1)} %layer.1) | data formatting | bytes 786432

commit v4 on v3

--- a/solution.py
+++ b/solution.py
@@ -1,4 +1,5 @@
 import functools
+import math
 
 import jax
 import jax.numpy as jnp
@@ -36,8 +37,8 @@
     ("s3", 5, 0), ("e2", 1, 3), ("e2", 2, 3), ("s4", 0, 0), ("s4", 1, 0), ("e1", 0, 0), ("e1", 1, 0), ("e1", 2, 0),
     ("e2", 0, 0), ("e2", 1, 0), ("e2", 2, 0),
 )
-N_SEND = 224
-N_RECV = 224
+N_SEND = 37
+N_RECV = 129
 
 
 def gelu(u):
@@ -55,7 +56,7 @@
     width,
     tok, gain, w_qkv, w_up, w_attn, w_down,
     out,
-    stats, statbuf, xraw, xbuf, w1buf, w2buf, pbuf, r1, r2, qkv, hbuf, obuf, osend, osib, ry1, ry2, xsend, xrecv,
+    stats, statbuf, xraw, xbuf, w1buf, w2buf, pbuf, r1, r2, qkv, hbuf, oall, osib, ry1, ry2, xsend, xrecv,
     send_sem, recv_sem,
 ):
     L, Y, C, H, Z = (lax.axis_index(a) for a in ("L", "Y", "C", "H", "Z"))
@@ -69,20 +70,24 @@
     straight = C == H
 
     count = {"s": 0, "r": 0}
-    pending = []
+    pending = {}
 
     def sems(kind, n=1):
         first = count[kind]
         count[kind] += n
         return first
 
-    def copy(src, dst, recv, dev):
-        d = pltpu.make_async_remote_copy(
-            src_ref=src, dst_ref=dst, send_sem=send_sem.at[sems("s")], recv_sem=recv_sem.at[recv],
+    def size(ref):
+        return math.prod(ref.shape) * 2
+
+    def copy(src, dst, recv, dev, kind):
+        if kind not in pending:
+            pending[kind] = [sems("s"), 0]
+        pending[kind][1] += size(src)
+        pltpu.make_async_remote_copy(
+            src_ref=src, dst_ref=dst, send_sem=send_sem.at[pending[kind][0]], recv_sem=recv_sem.at[recv],
             device_id=dev, device_id_type=MESH,
-        )
-        d.start()
-        pending.append(d)
+        ).start()
 
     def arrive(dst, recv):
         pltpu.make_async_remote_copy(
@@ -113,17 +118,17 @@
 
         unless(straight, dh + dl + dz == 0, greet)
 
-    w1_r = sems("r", 2 * CHUNKS)
-    w2_r = sems("r", 2 * PARTS)
+    w1_r = sems("r", CHUNKS)
+    w2_r = sems("r", PARTS)
 
     def send_w1(j, dev):
         block = w_qkv.at[j] if j < 3 else w_up.at[:, pl.ds((j - 3) * WIDE, WIDE)]
-        copy(block, w1buf.at[H, j], w1_r + H * CHUNKS + j, dev)
+        copy(block, w1buf.at[j, H], w1_r + j, dev, "w1")
 
     def send_w2(f, dev):
         top, columns = w_attn.shape[0], pl.ds(f * WIDE, WIDE)
-        copy(w_attn.at[:, columns], w2buf.at[H, f, pl.ds(0, top)], w2_r + H * PARTS + f, dev)
-        copy(w_down.at[:, columns], w2buf.at[H, f, pl.ds(top, w_down.shape[0])], w2_r + H * PARTS + f, dev)
+        copy(w_attn.at[:, columns], w2buf.at[H, f, pl.ds(0, top)], w2_r + f, dev, "w2")
+        copy(w_down.at[:, columns], w2buf.at[H, f, pl.ds(top, w_down.shape[0])], w2_r + f, dev, "w2")
 
     tokens_f = tok[...].astype(F32)
     lane = lax.broadcasted_iota(jnp.int32, (rows, 128), 1)
@@ -175,10 +180,10 @@
         xraw[L] = tok[...]
         statbuf[H, 0, 0] = stats[...]
 
-    yp_r, ym_r, ya_r, yb_r, sib_r = sems("r", 4), sems("r", 4), sems("r", 2), sems("r", 2), sems("r", 8)
+    yp_r, ym_r, far_r, sib_r = sems("r", 4), sems("r", 4), sems("r"), sems("r", 4)
 
     def to_sib(rel, b):
-        copy(xbuf.at[C, rel, b], xbuf.at[C, rel, b], sib_r + 2 * rel + b, sib)
+        copy(xbuf.at[C, rel, b], xbuf.at[C, rel, b], sib_r + rel, sib, "core")
 
     early = lax.rem(L + swapped, 2)
 
@@ -211,24 +216,24 @@
 
             at = slice(n * half, (n + 1) * half)
             xbuf[C, 0, b, part] = ((xraw[b, part].astype(F32) - mean[at]) * scale[at] * gains).astype(BF16)
-            copy(xbuf.at[C, 0, b, part], xbuf.at[C, 3, b, part], yp_r + 2 * b + n, up)
-            copy(xbuf.at[C, 0, b, part], xbuf.at[C, 1, b, part], ym_r + 2 * b + n, down)
+            copy(xbuf.at[C, 0, b, part], xbuf.at[C, 3, b, part], yp_r + 2 * b + n, up, "y")
+            copy(xbuf.at[C, 0, b, part], xbuf.at[C, 1, b, part], ym_r + 2 * b + n, down, "y")
         to_sib(0, b)
 
     def relay_y(b):
         arrive(xbuf.at[C, 3, b, first], yp_r + 2 * b)
-        copy(xbuf.at[C, 3, b, first], xbuf.at[C, 2, b, first], ya_r + b, up)
+        copy(xbuf.at[C, 3, b, first], xbuf.at[C, 2, b, first], far_r, up, "y")
         arrive(xbuf.at[C, 1, b, first], ym_r + 2 * b)
         arrive(xbuf.at[C, 1, b, second], ym_r + 2 * b + 1)
-        copy(xbuf.at[C, 1, b, second], xbuf.at[C, 2, b, second], yb_r + b, down)
+        copy(xbuf.at[C, 1, b, second], xbuf.at[C, 2, b, second], far_r, down, "y")
         to_sib(1, b)
         arrive(xbuf.at[C, 3, b, second], yp_r + 2 * b + 1)
         to_sib(3, b)
 
-    def far_y(b):
-        arrive(xbuf.at[C, 2, b, first], ya_r + b)
-        arrive(xbuf.at[C, 2, b, second], yb_r + b)
-        to_sib(2, b)
+    def far_y():
+        arrive(xbuf.at[C, 2], far_r)
+        for b in range(2):
+            to_sib(2, b)
 
     start_y(early)
     start_y(1 - early)
@@ -241,8 +246,8 @@
             send_w2(f, dev)
 
     n_items = 4 * CHUNKS
-    r1a_r, r1b_r, r2p_r, r2m_r = (sems("r", n_items) for _ in range(4))
-    dp_r, dm_r, da_r, db_r = (sems("r", 8) for _ in range(4))
+    r1_r, r2_r = sems("r", n_items), sems("r", n_items)
+    near_r, far_h = sems("r", 8), sems("r", 4)
     e_r = sems("r", 4 * PARTS)
     zp, zm, z2 = lax.rem(Z + 1, 4), lax.rem(Z + 3, 4), lax.rem(Z + 2, 4)
     seen_w, seen_x = set(), set()
@@ -251,38 +256,35 @@
         i = 4 * j + rel
         if j not in seen_w:
             seen_w.add(j)
-            for src in range(2):
-                arrive(w1buf.at[src, j], w1_r + src * CHUNKS + j)
+            arrive(w1buf.at[j], w1_r + j)
         if rel not in seen_x:
             seen_x.add(rel)
-            for b in range(2):
-                arrive(xbuf.at[1 - C, rel, b], sib_r + 2 * rel + b)
+            arrive(xbuf.at[1 - C, rel], sib_r + rel)
 
         @pl.loop(0, 2)
         def _(b):
-            acc = jnp.dot(xbuf[0, rel, b], w1buf[0, j], preferred_element_type=F32)
-            acc = acc + jnp.dot(xbuf[1, rel, b], w1buf[1, j], preferred_element_type=F32)
+            features = jnp.concatenate([xbuf[0, rel, b], xbuf[1, rel, b]], axis=1)
+            weights = w1buf[j].reshape(2 * feat, WIDE)
+            acc = jnp.dot(features, weights, preferred_element_type=F32)
             pbuf[i, b] = acc[:, :HEAD_DIM].astype(BF16)
             pbuf[i, 2 + b] = acc[:, HEAD_DIM:].astype(BF16)
 
-        copy(pbuf.at[i, z2, pl.ds(0, half)], r1.at[0, i], r1a_r + i, fwd)
-        copy(pbuf.at[i, z2, pl.ds(half, half)], r1.at[1, i], r1b_r + i, back)
+        copy(pbuf.at[i, z2, pl.ds(0, half)], r1.at[0, i], r1_r + i, fwd, "r1")
+        copy(pbuf.at[i, z2, pl.ds(half, half)], r1.at[1, i], r1_r + i, back, "r1")
 
     def s2(j, rel):
         i = 4 * j + rel
-        arrive(r1.at[0, i], r1a_r + i)
+        arrive(r1.at[:, i], r1_r + i)
         pbuf[i, zp, pl.ds(0, half)] = (pbuf[i, zp, pl.ds(0, half)].astype(F32) + r1[0, i].astype(F32)).astype(BF16)
-        copy(pbuf.at[i, zp], r2.at[0, i], r2p_r + i, fwd)
-        arrive(r1.at[1, i], r1b_r + i)
+        copy(pbuf.at[i, zp], r2.at[0, i], r2_r + i, fwd, "r2")
         pbuf[i, zm, pl.ds(half, half)] = (
             pbuf[i, zm, pl.ds(half, half)].astype(F32) + r1[1, i].astype(F32)
         ).astype(BF16)
-        copy(pbuf.at[i, zm], r2.at[1, i], r2m_r + i, back)
+        copy(pbuf.at[i, zm], r2.at[1, i], r2_r + i, back, "r2")
 
     def s3(j, rel):
         i = 4 * j + rel
-        arrive(r2.at[0, i], r2p_r + i)
-        arrive(r2.at[1, i], r2m_r + i)
+        arrive(r2.at[:, i], r2_r + i)
         whole = (pbuf[i, Z].astype(F32) + r2[0, i].astype(F32) + r2[1, i].astype(F32)).astype(BF16)
         if j < 3:
             qkv[rel, j] = whole
@@ -298,45 +300,37 @@
         if j in (3, 5):
             k = (j - 3) // 2
             mine = hbuf.at[rel, Z, pl.ds(2 * k, 2)]
-            copy(mine, mine, dp_r + 2 * rel + k, fwd)
-            copy(mine, mine, dm_r + 2 * rel + k, back)
+            copy(mine, mine, near_r + 2 * rel + k, fwd, "near")
+            copy(mine, mine, near_r + 2 * rel + k, back, "near")
 
     def relay(k, rel):
-        arrive(hbuf.at[rel, zm, pl.ds(2 * k, 2)], dp_r + 2 * rel + k)
+        arrive(hbuf.at[rel, pl.ds(0, 2), pl.ds(2 * k, 2)], near_r + 2 * rel + k)
         top = hbuf.at[rel, zm, pl.ds(2 * k, 2), pl.ds(0, half)]
-        copy(top, top, da_r + 2 * rel + k, fwd)
-        arrive(hbuf.at[rel, zp, pl.ds(2 * k, 2)], dm_r + 2 * rel + k)
+        copy(top, top, far_h + rel, fwd, "far")
         low = hbuf.at[rel, zp, pl.ds(2 * k, 2), pl.ds(half, half)]
-        copy(low, low, db_r + 2 * rel + k, back)
+        copy(low, low, far_h + rel, back, "far")
 
     seen_w2, seen_h = set(), set()
 
     def e1(f, rel):
         if f not in seen_w2:
             seen_w2.add(f)
-            for src in range(2):
-                arrive(w2buf.at[src, f], w2_r + src * PARTS + f)
+            arrive(w2buf.at[:, f], w2_r + f)
         if rel not in seen_h:
             seen_h.add(rel)
-            for k in range(2):
-                arrive(hbuf.at[rel, z2, pl.ds(2 * k, 2), pl.ds(0, half)], da_r + 2 * rel + k)
-                arrive(hbuf.at[rel, z2, pl.ds(2 * k, 2), pl.ds(half, half)], db_r + 2 * rel + k)
-
-        def product(side, b):
-            hidden = jnp.concatenate([hbuf[rel, 2 * h + b, k] for k in range(4) for h in range(2)], axis=1)
-            return jnp.dot(hidden, w2buf[side, f], preferred_element_type=F32).astype(BF16)
+            arrive(hbuf.at[rel, z2], far_h + rel)
 
         @pl.loop(0, 2)
         def _(b):
-            osend[rel, f, b] = product(1 - C, b)
-
-        copy(osend.at[rel, f], osib.at[rel, f], e_r + rel * PARTS + f, sib)
-
-        @pl.loop(0, 2)
-        def _(b):
-            obuf[rel, f, b] = product(C, b)
-
-    ry_r = sems("r", 4 * PARTS)
+            hidden = jnp.concatenate([hbuf[rel, 2 * h + b, k] for k in range(4) for h in range(2)], axis=1)
+            both = jnp.concatenate([w2buf[0, f], w2buf[1, f]], axis=1)
+            whole = jnp.dot(hidden, both, preferred_element_type=F32).astype(BF16)
+            for side in range(2):
+                oall[side, rel, f, b] = whole[:, side * WIDE : (side + 1) * WIDE]
+
+        copy(oall.at[1 - C, rel, f], osib.at[rel, f], e_r + rel * PARTS + f, sib, "cores")
+
+    ry_r = sems("r", 3 * PARTS)
     xr_r = sems("r", 2 * PARTS)
     xr_s = sems("s", 2 * PARTS)
 
@@ -348,9 +342,9 @@
 
     def e2(f, rel):
         arrive(osib.at[rel, f], e_r + rel * PARTS + f)
-        ry = ry_r + 4 * f
+        ry = ry_r + 3 * f
         for b in range(2):
-            total = obuf[rel, f, b].astype(F32) + osib[rel, f, b].astype(F32)
+            total = oall[C, rel, f, b].astype(F32) + osib[rel, f, b].astype(F32)
             if rel == 1 and b == 0:
                 arrive(ry1.at[f, 0], ry)
                 total = total + ry1[f, 0].astype(F32)
@@ -359,8 +353,7 @@
                 total = total + ry1[f, 1].astype(F32)
             if rel == 0:
                 if b == 0:
-                    arrive(ry2.at[f, 0], ry + 2)
-                    arrive(ry2.at[f, 1], ry + 3)
+                    arrive(ry2.at[f], ry + 2)
                 xsend[f, b] = (total + ry2[f, 0, b].astype(F32) + ry2[f, 1, b].astype(F32)).astype(BF16)
                 mine = jnp.logical_and(C == H, L == b)
 
@@ -372,19 +365,19 @@
                 def _():
                     final_copy(b, f).start()
             else:
-                obuf[rel, f, b] = total.astype(BF16)
+                oall[C, rel, f, b] = total.astype(BF16)
         if rel == 2:
-            copy(obuf.at[2, f, 0], ry1.at[f, 0], ry, up)
-            copy(obuf.at[2, f, 1], ry1.at[f, 1], ry + 1, down)
+            copy(oall.at[C, 2, f, 0], ry1.at[f, 0], ry, up, "ry1")
+            copy(oall.at[C, 2, f, 1], ry1.at[f, 1], ry + 1, down, "ry1")
         if rel == 1:
-            copy(obuf.at[1, f], ry2.at[f, 0], ry + 2, up)
+            copy(oall.at[C, 1, f], ry2.at[f, 0], ry + 2, up, "ry2")
         if rel == 3:
-            copy(obuf.at[3, f], ry2.at[f, 1], ry + 3, down)
+            copy(oall.at[C, 3, f], ry2.at[f, 1], ry + 2, down, "ry2")
 
     stages = {
         "y1": lambda a, rel: relay_y(early),
         "y2": lambda a, rel: relay_y(1 - early),
-        "y3": lambda a, rel: (far_y(early), far_y(1 - early)),
+        "y3": lambda a, rel: far_y(),
         "s1": s1, "s2": s2, "s3": s3, "s4": relay, "e1": e1, "e2": e2,
     }
     for stage, a, rel in ORDER:
@@ -404,8 +397,17 @@
 
     for n, r in enumerate(readers):
         unless(straight, r == (0, 0, 0), lambda: stat_copy(n).wait_send())
-    for d in pending:
-        d.wait_send()
+    whole = {
+        "w1": w1buf, "w2": w2buf, "y": xbuf.at[0, pl.ds(0, 3)], "core": xbuf.at[0], "r1": r1, "r2": r2,
+        "near": hbuf.at[pl.ds(0, 2)], "far": hbuf.at[0], "cores": osib, "ry1": ry1, "ry2": ry2,
+    }
+    for kind, (sem, total) in pending.items():
+        ref = whole[kind]
+        assert size(ref) == total, kind
+        pltpu.make_async_remote_copy(
+            src_ref=ref, dst_ref=ref, send_sem=send_sem.at[sem], recv_sem=recv_sem.at[0],
+            device_id=sib, device_id_type=MESH,
+        ).wait_send()
     for b in range(2):
 
         @pl.when(jnp.logical_not(jnp.logical_and(C == H, L == b)))
@@ -433,15 +435,14 @@
         vmem((2, 2, 4, 8, rows), F32),
         vmem((2, rows, feat), BF16),
         vmem((2, 4, 2, rows, feat), BF16),
-        vmem((2, CHUNKS, feat, WIDE), BF16),
+        vmem((CHUNKS, 2, feat, WIDE), BF16),
         vmem((2, PARTS, w_attn_out.shape[0] + w_down.shape[0], WIDE), BF16),
         vmem((n_items, 4, rows, HEAD_DIM), BF16),
         vmem((2, n_items, half, HEAD_DIM), BF16),
         vmem((2, n_items, rows, HEAD_DIM), BF16),
         vmem((4, 3, rows, HEAD_DIM), BF16),
         vmem((4, 4, 4, rows, HEAD_DIM), BF16),
-        vmem((4, *out_part), BF16),
-        vmem((4, *out_part), BF16),
+        vmem((2, 4, *out_part), BF16),
         vmem((4, *out_part), BF16),
         vmem((PARTS, 2, rows, WIDE), BF16),
         vmem((PARTS, 2, 2, rows, WIDE), BF16),

time: 155 us -> 152 us (0.981)
  Pallas kernels: 153 us -> 150 us
    pallas_call x1, Pallas kernels: 153 us -> 150 us  [local(): pl.pallas_call(functools.partial(kernel, width), out_shape=jax.ShapeDtype...]
where the time goes in v4:
time: 152 us
  Pallas kernels  150 us (99%)
  local copies, waits for them, and re-layouts  1.77 us (1%)
    pallas_call x1, Pallas kernels, local(): pl.pallas_call(functools.partial(kernel, width), out_shape=jax.ShapeDtype...  150 us

profile of v4, /device:TPU:1, one launch (start us, length us, event | category | flops | bytes accessed | tf_op | source)
XLA Modules:
  0.0 152.0 jit_solution(15288632035420424195)
XLA Ops:
  0.0 150.2 %layer.1 = bf16[256,768]{1,0:T(8,128)(2,1)} custom-call(bf16[256,768]{1,0:T(8,128)(2,1)} %tok.1, f32[768]{0:T(1024)} %gain.1, bf16[3,768,256]{2,1,0:T(8,128)(2,1)} %bitcast.1, bf16[768,768]{1,0:T(8,128)(2,1)} %w_up.1, bf16[256,768]{1,0:T(8,128)(2,1)} %w_attn.1, bf16[768,768]{1,0:T(8,128)(2,1)} %w_down.1), custom_call_target="tpu_custom_call" | custom-call | tf_op jit(solution)/shard_map/layer/pallas_call | solution.py:456
  150.2 1.8 %copy.8 = bf16[256,768]{1,0:T(8,128)(2,1)} copy(bf16[256,768]{1,0:T(8,128)(2,1)} %layer.1) | data formatting | bytes 786432

commit v5 on v4

--- a/solution.py
+++ b/solution.py
@@ -22,20 +22,20 @@
 WIDE = 2 * HEAD_DIM
 PARTS = 3
 ORDER = (
-    ("y1", 0, 0), ("s1", 0, 0), ("y2", 0, 0), ("s2", 0, 0), ("s3", 0, 0), ("s1", 1, 0), ("s1", 0, 1), ("s1", 1, 1),
-    ("s1", 0, 3), ("s1", 1, 3), ("s2", 1, 0), ("s2", 0, 1), ("s2", 1, 1), ("y3", 0, 0), ("s2", 0, 3), ("s2", 1, 3),
-    ("s3", 1, 0), ("s3", 0, 1), ("s1", 2, 1), ("s3", 1, 1), ("s1", 0, 2), ("s3", 0, 3), ("s1", 1, 2), ("s1", 2, 2),
-    ("s3", 1, 3), ("s1", 2, 3), ("s2", 2, 1), ("s2", 0, 2), ("s2", 1, 2), ("s2", 2, 2), ("s2", 2, 3), ("s3", 2, 1),
-    ("s3", 0, 2), ("s1", 3, 1), ("s3", 1, 2), ("s1", 3, 2), ("s3", 2, 2), ("s1", 3, 3), ("s3", 2, 3), ("s2", 3, 1),
-    ("s1", 4, 1), ("s2", 3, 2), ("s2", 3, 3), ("s3", 3, 1), ("s2", 4, 1), ("s3", 3, 2), ("s3", 3, 3), ("s4", 0, 1),
-    ("s3", 4, 1), ("s4", 0, 2), ("s1", 5, 1), ("s4", 0, 3), ("s1", 4, 2), ("s1", 5, 2), ("s2", 5, 1), ("s1", 4, 3),
-    ("s2", 4, 2), ("s2", 5, 2), ("s3", 5, 1), ("s2", 4, 3), ("s3", 4, 2), ("s3", 5, 2), ("s4", 1, 1), ("s3", 4, 3),
-    ("s1", 2, 0), ("s1", 5, 3), ("s4", 1, 2), ("e1", 0, 1), ("e1", 1, 1), ("s2", 2, 0), ("s2", 5, 3), ("e1", 0, 2),
-    ("e1", 2, 1), ("e1", 1, 2), ("e2", 0, 2), ("s3", 2, 0), ("s3", 5, 3), ("e1", 2, 2), ("e2", 1, 2), ("s1", 3, 0),
-    ("e2", 2, 2), ("s1", 4, 0), ("s1", 5, 0), ("e2", 0, 1), ("s4", 1, 3), ("s2", 3, 0), ("s2", 4, 0), ("e2", 1, 1),
-    ("s2", 5, 0), ("e1", 0, 3), ("e2", 2, 1), ("s3", 3, 0), ("e1", 1, 3), ("s3", 4, 0), ("e2", 0, 3), ("e1", 2, 3),
-    ("s3", 5, 0), ("e2", 1, 3), ("e2", 2, 3), ("s4", 0, 0), ("s4", 1, 0), ("e1", 0, 0), ("e1", 1, 0), ("e1", 2, 0),
-    ("e2", 0, 0), ("e2", 1, 0), ("e2", 2, 0),
+    ("y1", 0, 0), ("s1", 0, 0), ("y2", 0, 0), ("s2", 0, 0), ("s1", 1, 0), ("s1", 0, 1), ("s1", 1, 1), ("s1", 0, 3),
+    ("s2", 1, 0), ("s1", 1, 3), ("s2", 0, 1), ("s2", 0, 3), ("y3", 0, 0), ("s1", 2, 2), ("s1", 1, 2), ("s2", 1, 1),
+    ("s2", 1, 3), ("s1", 0, 2), ("s1", 2, 1), ("s1", 2, 3), ("s2", 1, 2), ("s2", 2, 2), ("s1", 3, 2), ("s2", 0, 2),
+    ("s2", 2, 1), ("s2", 3, 2), ("s1", 3, 1), ("s3", 0, 1), ("s3", 0, 2), ("s3", 1, 2), ("s3", 0, 3), ("s1", 3, 3),
+    ("s2", 2, 3), ("s3", 1, 3), ("s3", 2, 2), ("s1", 4, 3), ("s1", 3, 0), ("s2", 3, 1), ("s3", 1, 1), ("s1", 4, 2),
+    ("s1", 4, 1), ("s2", 4, 3), ("s3", 3, 2), ("s1", 5, 2), ("s1", 5, 3), ("s2", 4, 1), ("s3", 2, 1), ("s1", 5, 1),
+    ("s2", 4, 2), ("s3", 2, 3), ("s2", 5, 2), ("s2", 5, 3), ("s4", 0, 2), ("s3", 4, 2), ("s2", 3, 3), ("s2", 5, 1),
+    ("s3", 5, 2), ("s3", 3, 3), ("s3", 3, 1), ("s3", 4, 1), ("s3", 4, 3), ("s4", 1, 2), ("s3", 5, 1), ("s3", 5, 3),
+    ("s1", 4, 0), ("s3", 0, 0), ("s1", 2, 0), ("e1", 0, 2), ("s4", 0, 1), ("s4", 1, 1), ("s4", 1, 3), ("e1", 1, 2),
+    ("s1", 5, 0), ("s3", 1, 0), ("e2", 0, 2), ("e1", 2, 2), ("s4", 0, 3), ("s2", 2, 0), ("e2", 1, 2), ("s2", 3, 0),
+    ("e1", 1, 1), ("e1", 0, 1), ("s2", 4, 0), ("e2", 2, 2), ("e1", 0, 3), ("s2", 5, 0), ("s3", 2, 0), ("s3", 3, 0),
+    ("e2", 0, 1), ("e2", 0, 3), ("e2", 1, 1), ("s3", 4, 0), ("s3", 5, 0), ("e1", 1, 3), ("e2", 1, 3), ("e1", 2, 1),
+    ("s4", 0, 0), ("e1", 2, 3), ("s4", 1, 0), ("e2", 2, 1), ("e2", 2, 3), ("e1", 0, 0), ("e1", 1, 0), ("e2", 0, 0),
+    ("e1", 2, 0), ("e2", 1, 0), ("e2", 2, 0),
 )
 N_SEND = 37
 N_RECV = 129

time: 152 us -> 147 us (0.967)
  Pallas kernels: 150 us -> 145 us
    pallas_call x1, Pallas kernels: 150 us -> 145 us  [local(): pl.pallas_call(functools.partial(kernel, width), out_shape=jax.ShapeDtype...]
where the time goes in v5:
time: 147 us; the launch traced here: 146 us
  Pallas kernels  145 us (99%)
  local copies, waits for them, and re-layouts  1.77 us (1%)
    pallas_call x1, Pallas kernels, local(): pl.pallas_call(functools.partial(kernel, width), out_shape=jax.ShapeDtype...  145 us

profile of v5, /device:TPU:1, one launch (start us, length us, event | category | flops | bytes accessed | tf_op | source)
XLA Modules:
  0.0 146.4 jit_solution(13246830204749958289)
XLA Ops:
  0.0 144.7 %layer.1 = bf16[256,768]{1,0:T(8,128)(2,1)} custom-call(bf16[256,768]{1,0:T(8,128)(2,1)} %tok.1, f32[768]{0:T(1024)} %gain.1, bf16[3,768,256]{2,1,0:T(8,128)(2,1)} %bitcast.1, bf16[768,768]{1,0:T(8,128)(2,1)} %w_up.1, bf16[256,768]{1,0:T(8,128)(2,1)} %w_attn.1, bf16[768,768]{1,0:T(8,128)(2,1)} %w_down.1), custom_call_target="tpu_custom_call" | custom-call | tf_op jit(solution)/shard_map/layer/pallas_call | solution.py:456
  144.7 1.8 %copy.8 = bf16[256,768]{1,0:T(8,128)(2,1)} copy(bf16[256,768]{1,0:T(8,128)(2,1)} %layer.1) | data formatting | bytes 786432

commit v6 on v5

--- a/solution.py
+++ b/solution.py
@@ -22,20 +22,20 @@
 WIDE = 2 * HEAD_DIM
 PARTS = 3
 ORDER = (
-    ("y1", 0, 0), ("s1", 0, 0), ("y2", 0, 0), ("s2", 0, 0), ("s1", 1, 0), ("s1", 0, 1), ("s1", 1, 1), ("s1", 0, 3),
-    ("s2", 1, 0), ("s1", 1, 3), ("s2", 0, 1), ("s2", 0, 3), ("y3", 0, 0), ("s1", 2, 2), ("s1", 1, 2), ("s2", 1, 1),
-    ("s2", 1, 3), ("s1", 0, 2), ("s1", 2, 1), ("s1", 2, 3), ("s2", 1, 2), ("s2", 2, 2), ("s1", 3, 2), ("s2", 0, 2),
-    ("s2", 2, 1), ("s2", 3, 2), ("s1", 3, 1), ("s3", 0, 1), ("s3", 0, 2), ("s3", 1, 2), ("s3", 0, 3), ("s1", 3, 3),
-    ("s2", 2, 3), ("s3", 1, 3), ("s3", 2, 2), ("s1", 4, 3), ("s1", 3, 0), ("s2", 3, 1), ("s3", 1, 1), ("s1", 4, 2),
-    ("s1", 4, 1), ("s2", 4, 3), ("s3", 3, 2), ("s1", 5, 2), ("s1", 5, 3), ("s2", 4, 1), ("s3", 2, 1), ("s1", 5, 1),
-    ("s2", 4, 2), ("s3", 2, 3), ("s2", 5, 2), ("s2", 5, 3), ("s4", 0, 2), ("s3", 4, 2), ("s2", 3, 3), ("s2", 5, 1),
-    ("s3", 5, 2), ("s3", 3, 3), ("s3", 3, 1), ("s3", 4, 1), ("s3", 4, 3), ("s4", 1, 2), ("s3", 5, 1), ("s3", 5, 3),
-    ("s1", 4, 0), ("s3", 0, 0), ("s1", 2, 0), ("e1", 0, 2), ("s4", 0, 1), ("s4", 1, 1), ("s4", 1, 3), ("e1", 1, 2),
-    ("s1", 5, 0), ("s3", 1, 0), ("e2", 0, 2), ("e1", 2, 2), ("s4", 0, 3), ("s2", 2, 0), ("e2", 1, 2), ("s2", 3, 0),
-    ("e1", 1, 1), ("e1", 0, 1), ("s2", 4, 0), ("e2", 2, 2), ("e1", 0, 3), ("s2", 5, 0), ("s3", 2, 0), ("s3", 3, 0),
-    ("e2", 0, 1), ("e2", 0, 3), ("e2", 1, 1), ("s3", 4, 0), ("s3", 5, 0), ("e1", 1, 3), ("e2", 1, 3), ("e1", 2, 1),
-    ("s4", 0, 0), ("e1", 2, 3), ("s4", 1, 0), ("e2", 2, 1), ("e2", 2, 3), ("e1", 0, 0), ("e1", 1, 0), ("e2", 0, 0),
-    ("e1", 2, 0), ("e2", 1, 0), ("e2", 2, 0),
+    ("y1", 0, 0), ("s1", 0, 0), ("y2", 0, 0), ("s2", 0, 0), ("s1", 1, 0), ("s1", 0, 1), ("s1", 1, 3), ("s1", 1, 1),
+    ("s2", 1, 0), ("s1", 0, 3), ("s2", 0, 1), ("s2", 1, 3), ("s1", 2, 3), ("s2", 1, 1), ("s2", 0, 3), ("y3", 0, 0),
+    ("s1", 2, 2), ("s2", 2, 3), ("s1", 1, 2), ("s1", 0, 2), ("s1", 2, 1), ("s2", 2, 2), ("s3", 0, 1), ("s1", 3, 3),
+    ("s1", 3, 2), ("s3", 1, 1), ("s1", 3, 1), ("s2", 0, 2), ("s2", 2, 1), ("s2", 1, 2), ("s2", 3, 1), ("s2", 3, 3),
+    ("s1", 4, 1), ("s3", 0, 3), ("s1", 4, 2), ("s3", 0, 2), ("s1", 4, 3), ("s3", 1, 2), ("s3", 2, 1), ("s1", 2, 0),
+    ("s3", 3, 1), ("s2", 3, 2), ("s3", 2, 2), ("s2", 4, 3), ("s1", 5, 1), ("s1", 5, 2), ("s2", 4, 2), ("s3", 3, 2),
+    ("s3", 1, 3), ("s3", 2, 3), ("s2", 5, 2), ("s2", 5, 1), ("s3", 3, 3), ("s4", 0, 2), ("s2", 4, 1), ("s1", 5, 3),
+    ("s3", 4, 2), ("s3", 5, 2), ("s1", 4, 0), ("s1", 5, 0), ("s1", 3, 0), ("s2", 5, 3), ("s3", 4, 1), ("s3", 5, 1),
+    ("s4", 1, 2), ("s3", 4, 3), ("s3", 5, 3), ("s4", 1, 1), ("e1", 1, 2), ("s4", 0, 1), ("s3", 0, 0), ("s4", 0, 3),
+    ("s4", 1, 3), ("e2", 1, 2), ("e1", 0, 2), ("s2", 2, 0), ("e1", 2, 2), ("s2", 3, 0), ("s2", 4, 0), ("s2", 5, 0),
+    ("s3", 1, 0), ("e2", 0, 2), ("e1", 0, 1), ("e1", 1, 1), ("e2", 2, 2), ("e1", 0, 3), ("e1", 2, 1), ("s3", 2, 0),
+    ("s3", 3, 0), ("e2", 1, 1), ("e2", 0, 1), ("e2", 0, 3), ("s3", 4, 0), ("s3", 5, 0), ("e1", 1, 3), ("e1", 2, 3),
+    ("e2", 1, 3), ("s4", 0, 0), ("e2", 2, 1), ("s4", 1, 0), ("e2", 2, 3), ("e1", 1, 0), ("e2", 1, 0), ("e1", 0, 0),
+    ("e2", 0, 0), ("e1", 2, 0), ("e2", 2, 0),
 )
 N_SEND = 37
 N_RECV = 129

time: 147 us -> 146 us (level)
  no operation moved by 1% of the time
where the time goes in v6:
time: 146 us
  Pallas kernels  144 us (99%)
  local copies, waits for them, and re-layouts  1.77 us (1%)
    pallas_call x1, Pallas kernels, local(): pl.pallas_call(functools.partial(kernel, width), out_shape=jax.ShapeDtype...  144 us

profile of v6, /device:TPU:1, one launch (start us, length us, event | category | flops | bytes accessed | tf_op | source)
XLA Modules:
  0.0 145.6 jit_solution(952177165531598378)
XLA Ops:
  0.0 143.8 %layer.1 = bf16[256,768]{1,0:T(8,128)(2,1)} custom-call(bf16[256,768]{1,0:T(8,128)(2,1)} %tok.1, f32[768]{0:T(1024)} %gain.1, bf16[3,768,256]{2,1,0:T(8,128)(2,1)} %bitcast.1, bf16[768,768]{1,0:T(8,128)(2,1)} %w_up.1, bf16[256,768]{1,0:T(8,128)(2,1)} %w_attn.1, bf16[768,768]{1,0:T(8,128)(2,1)} %w_down.1), custom_call_target="tpu_custom_call" | custom-call | tf_op jit(solution)/shard_map/layer/pallas_call | solution.py:456
  143.8 1.8 %copy.8 = bf16[256,768]{1,0:T(8,128)(2,1)} copy(bf16[256,768]{1,0:T(8,128)(2,1)} %layer.1) | data formatting | bytes 786432

commit v7 on v6

--- a/solution.py
+++ b/solution.py
@@ -23,14 +23,14 @@
 PARTS = 3
 ORDER = (
     ("y1", 0, 0), ("s1", 0, 0), ("y2", 0, 0), ("s2", 0, 0), ("s1", 1, 0), ("s1", 0, 1), ("s1", 1, 3), ("s1", 1, 1),
-    ("s2", 1, 0), ("s1", 0, 3), ("s2", 0, 1), ("s2", 1, 3), ("s1", 2, 3), ("s2", 1, 1), ("s2", 0, 3), ("y3", 0, 0),
+    ("s2", 1, 0), ("s1", 0, 3), ("s2", 0, 1), ("s2", 1, 3), ("s1", 2, 3), ("y3", 0, 0), ("s2", 1, 1), ("s2", 0, 3),
     ("s1", 2, 2), ("s2", 2, 3), ("s1", 1, 2), ("s1", 0, 2), ("s1", 2, 1), ("s2", 2, 2), ("s3", 0, 1), ("s1", 3, 3),
     ("s1", 3, 2), ("s3", 1, 1), ("s1", 3, 1), ("s2", 0, 2), ("s2", 2, 1), ("s2", 1, 2), ("s2", 3, 1), ("s2", 3, 3),
     ("s1", 4, 1), ("s3", 0, 3), ("s1", 4, 2), ("s3", 0, 2), ("s1", 4, 3), ("s3", 1, 2), ("s3", 2, 1), ("s1", 2, 0),
     ("s3", 3, 1), ("s2", 3, 2), ("s3", 2, 2), ("s2", 4, 3), ("s1", 5, 1), ("s1", 5, 2), ("s2", 4, 2), ("s3", 3, 2),
     ("s3", 1, 3), ("s3", 2, 3), ("s2", 5, 2), ("s2", 5, 1), ("s3", 3, 3), ("s4", 0, 2), ("s2", 4, 1), ("s1", 5, 3),
     ("s3", 4, 2), ("s3", 5, 2), ("s1", 4, 0), ("s1", 5, 0), ("s1", 3, 0), ("s2", 5, 3), ("s3", 4, 1), ("s3", 5, 1),
-    ("s4", 1, 2), ("s3", 4, 3), ("s3", 5, 3), ("s4", 1, 1), ("e1", 1, 2), ("s4", 0, 1), ("s3", 0, 0), ("s4", 0, 3),
+    ("s4", 1, 2), ("s3", 4, 3), ("s3", 5, 3), ("s4", 1, 1), ("s4", 0, 1), ("s3", 0, 0), ("s4", 0, 3), ("e1", 1, 2),
     ("s4", 1, 3), ("e2", 1, 2), ("e1", 0, 2), ("s2", 2, 0), ("e1", 2, 2), ("s2", 3, 0), ("s2", 4, 0), ("s2", 5, 0),
     ("s3", 1, 0), ("e2", 0, 2), ("e1", 0, 1), ("e1", 1, 1), ("e2", 2, 2), ("e1", 0, 3), ("e1", 2, 1), ("s3", 2, 0),
     ("s3", 3, 0), ("e2", 1, 1), ("e2", 0, 1), ("e2", 0, 3), ("s3", 4, 0), ("s3", 5, 0), ("e1", 1, 3), ("e1", 2, 3),

time: 146 us -> 146 us (level)
  no operation moved by 1% of the time
where the time goes in v7:
time: 146 us
  Pallas kernels  144 us (99%)
  local copies, waits for them, and re-layouts  1.77 us (1%)
    pallas_call x1, Pallas kernels, local(): pl.pallas_call(functools.partial(kernel, width), out_shape=jax.ShapeDtype...  144 us

profile of v7, /device:TPU:1, one launch (start us, length us, event | category | flops | bytes accessed | tf_op | source)
XLA Modules:
  0.0 145.6 jit_solution(13805958177019978111)
XLA Ops:
  0.0 143.8 %layer.1 = bf16[256,768]{1,0:T(8,128)(2,1)} custom-call(bf16[256,768]{1,0:T(8,128)(2,1)} %tok.1, f32[768]{0:T(1024)} %gain.1, bf16[3,768,256]{2,1,0:T(8,128)(2,1)} %bitcast.1, bf16[768,768]{1,0:T(8,128)(2,1)} %w_up.1, bf16[256,768]{1,0:T(8,128)(2,1)} %w_attn.1, bf16[768,768]{1,0:T(8,128)(2,1)} %w_down.1), custom_call_target="tpu_custom_call" | custom-call | tf_op jit(solution)/shard_map/layer/pallas_call | solution.py:456
  143.8 1.8 %copy.8 = bf16[256,768]{1,0:T(8,128)(2,1)} copy(bf16[256,768]{1,0:T(8,128)(2,1)} %layer.1) | data formatting | bytes 786432

commit v8 on v7

--- a/solution.py
+++ b/solution.py
@@ -30,8 +30,8 @@
     ("s3", 3, 1), ("s2", 3, 2), ("s3", 2, 2), ("s2", 4, 3), ("s1", 5, 1), ("s1", 5, 2), ("s2", 4, 2), ("s3", 3, 2),
     ("s3", 1, 3), ("s3", 2, 3), ("s2", 5, 2), ("s2", 5, 1), ("s3", 3, 3), ("s4", 0, 2), ("s2", 4, 1), ("s1", 5, 3),
     ("s3", 4, 2), ("s3", 5, 2), ("s1", 4, 0), ("s1", 5, 0), ("s1", 3, 0), ("s2", 5, 3), ("s3", 4, 1), ("s3", 5, 1),
-    ("s4", 1, 2), ("s3", 4, 3), ("s3", 5, 3), ("s4", 1, 1), ("s4", 0, 1), ("s3", 0, 0), ("s4", 0, 3), ("e1", 1, 2),
-    ("s4", 1, 3), ("e2", 1, 2), ("e1", 0, 2), ("s2", 2, 0), ("e1", 2, 2), ("s2", 3, 0), ("s2", 4, 0), ("s2", 5, 0),
+    ("s4", 1, 2), ("s3", 4, 3), ("s3", 5, 3), ("s4", 1, 1), ("s4", 0, 1), ("s3", 0, 0), ("s4", 0, 3), ("s4", 1, 3),
+    ("e1", 1, 2), ("e2", 1, 2), ("e1", 0, 2), ("s2", 2, 0), ("e1", 2, 2), ("s2", 3, 0), ("s2", 4, 0), ("s2", 5, 0),
     ("s3", 1, 0), ("e2", 0, 2), ("e1", 0, 1), ("e1", 1, 1), ("e2", 2, 2), ("e1", 0, 3), ("e1", 2, 1), ("s3", 2, 0),
     ("s3", 3, 0), ("e2", 1, 1), ("e2", 0, 1), ("e2", 0, 3), ("s3", 4, 0), ("s3", 5, 0), ("e1", 1, 3), ("e1", 2, 3),
     ("e2", 1, 3), ("s4", 0, 0), ("e2", 2, 1), ("s4", 1, 0), ("e2", 2, 3), ("e1", 1, 0), ("e2", 1, 0), ("e1", 0, 0),

time: 146 us -> 148 us (1.014)
  Pallas kernels: 144 us -> 146 us
    pallas_call x1, Pallas kernels: 144 us -> 146 us  [local(): pl.pallas_call(functools.partial(kernel, width), out_shape=jax.ShapeDtype...]
where the time goes in v8:
time: 148 us; the launch traced here: 147 us
  Pallas kernels  146 us (99%)
  local copies, waits for them, and re-layouts  1.77 us (1%)
    pallas_call x1, Pallas kernels, local(): pl.pallas_call(functools.partial(kernel, width), out_shape=jax.ShapeDtype...  146 us

profile of v8, /device:TPU:1, one launch (start us, length us, event | category | flops | bytes accessed | tf_op | source)
XLA Modules:
  0.0 147.5 jit_solution(8029046089722709704)
XLA Ops:
  0.0 145.7 %layer.1 = bf16[256,768]{1,0:T(8,128)(2,1)} custom-call(bf16[256,768]{1,0:T(8,128)(2,1)} %tok.1, f32[768]{0:T(1024)} %gain.1, bf16[3,768,256]{2,1,0:T(8,128)(2,1)} %bitcast.1, bf16[768,768]{1,0:T(8,128)(2,1)} %w_up.1, bf16[256,768]{1,0:T(8,128)(2,1)} %w_attn.1, bf16[768,768]{1,0:T(8,128)(2,1)} %w_down.1), custom_call_target="tpu_custom_call" | custom-call | tf_op jit(solution)/shard_map/layer/pallas_call | solution.py:456
  145.7 1.8 %copy.8 = bf16[256,768]{1,0:T(8,128)(2,1)} copy(bf16[256,768]{1,0:T(8,128)(2,1)} %layer.1) | data formatting | bytes 786432
